TPU v7x, 128 devices: a whole 4x4x4 slice. The times are simulated.
128 devices in a mesh: row: 32 (over x, z, y_lo), col: 4 (over y_hi, core).
Axes of the slice: x: 4, y: 4 (y_hi: 2, y_lo: 2; y = y_hi * 2 + y_lo), z: 4, core: 2. Of those that a mesh axis runs over, the one named last changes fastest.
Arguments:
- pair: bfloat16 [1536, 1536, 128], P('row', 'col'), may hold values from -6 to 6
- gain_in: float32 [128], replicated, may hold values from 0.25 to 1.75
- w_a_gate: bfloat16 [128, 128], replicated, may hold values from -0.5 to 0.5
- w_a: bfloat16 [128, 128], replicated, may hold values from -0.5 to 0.5
- w_b_gate: bfloat16 [128, 128], replicated, may hold values from -0.5 to 0.5
- w_b: bfloat16 [128, 128], replicated, may hold values from -0.5 to 0.5
- w_out_gate: bfloat16 [128, 128], replicated, may hold values from -0.5 to 0.5
- w_out: bfloat16 [128, 128], replicated, may hold values from -0.5 to 0.5
- gain_out: float32 [128], replicated, may hold values from 0.25 to 1.75
Outputs:
- update: bfloat16 [1536, 1536, 128], P('row', 'col')
All inputs are finite; a program needn't handle non-finite values.
Results may differ from a plain program's by a relative error of at most 0.0083.
Values may be sent and summed in bfloat16 or wider, within the bound.
No kernel may reach another device: no remote copies, remote signals or barrier semaphores. Data moves between devices by JAX's collectives and lax.ppermute only.
A program may use at most 128 MiB of HBM per device.

v0:
```python
import jax
import jax.numpy as jnp
from jax import lax
from jax.sharding import PartitionSpec as P


def cut_along(array, dim, count):
    shape = array.shape
    parts = array.reshape(*shape[:dim], count, shape[dim] // count, *shape[dim + 1 :])
    return jnp.moveaxis(parts, dim, 0)


def laid_out(parts, dim):
    parts = jnp.moveaxis(parts, 0, dim)
    shape = parts.shape
    return parts.reshape(*shape[:dim], shape[dim] * shape[dim + 1], *shape[dim + 2 :])


def one_exchange(array, axis, axes, splits, concats):
    sizes = [lax.axis_size(a) for a in axes]
    parts = cut_along(array, splits[0], sizes[0])
    parts = jnp.moveaxis(cut_along(parts, splits[1] + 1, sizes[1]), 0, 1)
    inside = parts.shape[2:]
    parts = parts.reshape(-1, *inside)
    parts = lax.all_to_all(parts, axis, split_axis=0, concat_axis=0, tiled=True)
    parts = laid_out(parts.reshape(*sizes, *inside), concats[0] + 1)
    return laid_out(parts, concats[1])


def layer_norm_last(values, gain):
    centred = values - jnp.mean(values, axis=-1, keepdims=True)
    variance = jnp.mean(centred * centred, axis=-1, keepdims=True)
    return centred * lax.rsqrt(variance + 1e-05) * gain


def project_major(normed, weight):
    return jnp.einsum("ijd,de->eij", normed, weight, preferred_element_type=jnp.float32)


def local(pair, gain_in, w_a_gate, w_a, w_b_gate, w_b, w_out_gate, w_out, gain_out):
    channels = w_out.shape[0]
    normed = layer_norm_last(pair.astype(jnp.float32), gain_in).astype(jnp.bfloat16)
    left = (jax.nn.sigmoid(project_major(normed, w_a_gate)) * project_major(normed, w_a)).astype(
        jnp.bfloat16
    )
    right = (jax.nn.sigmoid(project_major(normed, w_b_gate)) * project_major(normed, w_b)).astype(
        jnp.bfloat16
    )
    gating = jax.nn.sigmoid(
        jnp.einsum("ijd,de->ije", normed, w_out_gate, preferred_element_type=jnp.float32)
    )
    left_owned, right_owned = (
        one_exchange(left, ("row", "col"), ("row", "col"), (0, 0), (1, 2)),
        one_exchange(right, ("row", "col"), ("row", "col"), (0, 0), (1, 2)),
    )
    summed = jnp.einsum(
        "cki,ckj->cij", left_owned, right_owned, preferred_element_type=jnp.float32
    ).astype(jnp.bfloat16)
    returned = one_exchange(summed, ("row", "col"), ("row", "col"), (1, 2), (0, 0))
    row_count = lax.axis_size("row")
    col_count = lax.axis_size("col")
    per_device = channels // (row_count * col_count)
    gain_used = (
        gain_out.reshape(row_count, col_count, per_device).transpose(1, 0, 2).reshape(channels)
    )
    weight_used = (
        w_out.reshape(row_count, col_count, per_device, channels)
        .transpose(1, 0, 2, 3)
        .reshape(channels, channels)
    )
    values = returned.astype(jnp.float32)
    centred = values - jnp.mean(values, axis=0, keepdims=True)
    variance = jnp.mean(centred * centred, axis=0, keepdims=True)
    scaled = (centred * lax.rsqrt(variance + 1e-05) * gain_used[:, None, None]).astype(jnp.bfloat16)
    projected = jnp.einsum("cij,cd->ijd", scaled, weight_used, preferred_element_type=jnp.float32)
    return (gating * projected).astype(jnp.bfloat16)


def solution(mesh):
    in_specs = (P("row", "col", None), P(), P(), P(), P(), P(), P(), P(), P())
    out_specs = P("row", "col", None)
    return jax.shard_map(local, mesh=mesh, in_specs=in_specs, out_specs=out_specs, check_vma=False)
```

profile of v0, /device:TPU:1, one launch (start us, length us, event | category | flops | bytes accessed | tf_op | source)
XLA Modules:
  0.0 297.9 jit_solution(11252400598608413234)
XLA Ops:
  0.0 0.0 copy-start
  0.0 0.0 copy-start.2
  0.0 0.0 copy-start.5
  0.0 3.8 %convert_reduce_fusion = f32[48,384]{1,0:T(8,128)S(1)} fusion(bf16[48,384,128]{2,1,0:T(8,128)(2,1)} %param.9), kind=kLoop, calls=%fused_computation.1 | loop fusion | flops 4700160 | bytes 4792320 | tf_op jit(solution)/shard_map/reduce_sum | solution.py:31
  3.8 7.1 %fusion.2 = f32[48,384]{1,0:T(8,128)S(1)} fusion(bf16[48,384,128]{2,1,0:T(8,128)(2,1)} %param.9, f32[48,384]{1,0:T(8,128)S(1)} %broadcast_multiply_fusion.1), kind=kLoop, calls=%fused_computation.4 | loop fusion | flops 9418752 | bytes 4866048 | tf_op jit(solution)/shard_map/reduce_sum | solution.py:32
  11.0 0.0 copy-done
  11.0 0.0 copy-done.2
  11.0 0.0 copy-done.5
  11.0 0.0 copy-start.7
  11.0 5.1 %fusion.20 = f32[48,384,128]{2,1,0:T(8,128)S(1)} fusion(bf16[128,128]{1,0:T(8,128)(2,1)S(1)} %copy-done, bf16[48,384,128]{2,1,0:T(8,128)(2,1)S(1)} %copy-done.2, f32[128]{0:T(128)S(1)} %copy-done.5, f32[48,384]{1,0:T(8,128)S(1)} %add_rsqrt_fusion.1, f32[48,384]{1,0:T(8,128)S(1)} %broadcast_multiply_fusion.1), kind=kOutput, calls=%fused_computation.31 | convolution fusion | flops 615776256 | bytes 14336512 | tf_op jit(solution)/shard_map/ijd,de->eij/dot_general | solution.py:37
  16.1 0.0 copy-done.7
  16.1 9.2 %fusion.17 = bf16[128,1,48,384]{0,3,2,1:T(8,128)(2,1)} fusion(f32[48,384,128]{2,1,0:T(8,128)S(1)} %fusion.20, bf16[128,128]{1,0:T(8,128)(2,1)S(1)} %copy-done.7, bf16[48,384,128]{2,1,0:T(8,128)(2,1)S(1)} %copy-done.2, f32[128]{0:T(128)S(1)} %copy-done.5, f32[48,384]{1,0:T(8,128)S(1)} %add_rsqrt_fusion.1, f32[48,384]{1,0:T(8,128)S(1)} %broadcast_multiply_fusion.1), kind=kOutput, calls=%fused_computation.24 | convolution fusion | flops 627572736 | bytes 19055104 | tf_op jit(solution)/shard_map/ijd,de->eij/dot_general | solution.py:37
  25.3 0.0 copy-start.3
  25.3 7.2 %copy.26 = bf16[128,1,48,384]{3,2,1,0:T(8,128)(2,1)} copy(bf16[128,1,48,384]{0,3,2,1:T(8,128)(2,1)} %fusion.17) | data formatting | bytes 9437184 | tf_op jit(solution)/shard_map/reshape;reshape;reshape | solution.py:24
  32.5 0.0 slice-start
  32.5 11.9 %all-to-all-start.1 = ((bf16[128,1,48,384]{3,2,1,0:T(8,128)(2,1)}), bf16[128,1,48,384]{3,2,1,0:T(8,128)(2,1)}, u32[]{:S(2)}, u32[]{:S(2)}) async-start(bf16[128,1,48,384]{3,2,1,0:T(8,128)(2,1)} %copy.26), calls=%async_computation.1 | async-start | bytes 9437184 | tf_op jit(solution)/shard_map/all_to_all | solution.py:25
  44.4 0.0 copy-done.3
  44.4 0.0 slice-start.1
  44.4 0.0 copy-start.8
  44.4 9.5 %fusion.23 = f32[48,384,128]{2,1,0:T(8,128)S(1)} fusion(bf16[128,128]{1,0:T(8,128)(2,1)S(1)} %copy-done.3, bf16[48,384,128]{2,1,0:T(8,128)(2,1)} %param.9, f32[128]{0:T(128)S(1)} %copy-done.5, f32[48,384]{1,0:T(8,128)S(1)} %add_rsqrt_fusion.1, f32[48,384]{1,0:T(8,128)S(1)} %broadcast_multiply_fusion.1), kind=kOutput, calls=%fused_computation.34 | convolution fusion | flops 615776256 | bytes 14336512 | tf_op jit(solution)/shard_map/ijd,de->eij/dot_general | solution.py:37
  53.9 0.0 slice-done
  53.9 0.0 slice-done.1
  53.9 0.0 copy-done.8
  53.9 9.2 %fusion.16 = bf16[128,1,48,384]{0,3,2,1:T(8,128)(2,1)} fusion(f32[48,384,128]{2,1,0:T(8,128)S(1)} %fusion.23, bf16[128,128]{1,0:T(8,128)(2,1)S(1)} %copy-done.8, bf16[48,384,128]{2,1,0:T(8,128)(2,1)S(1)} %bitcast.85, f32[128]{0:T(128)S(1)} %copy-done.5, f32[48,384]{1,0:T(8,128)S(1)} %add_rsqrt_fusion.1, f32[48,384]{1,0:T(8,128)S(1)} %broadcast_multiply_fusion.1), kind=kOutput, calls=%fused_computation.23 | convolution fusion | flops 627572736 | bytes 19055104 | tf_op jit(solution)/shard_map/ijd,de->eij/dot_general | solution.py:37
  63.1 7.0 %copy.23 = bf16[128,1,48,384]{3,2,1,0:T(8,128)(2,1)} copy(bf16[128,1,48,384]{0,3,2,1:T(8,128)(2,1)} %fusion.16) | data formatting | bytes 9437184 | tf_op jit(solution)/shard_map/reshape;reshape;reshape | solution.py:24
  70.1 33.4 %all-to-all-done.1 = bf16[128,1,48,384]{3,2,1,0:T(8,128)(2,1)} async-done(((bf16[128,1,48,384]{3,2,1,0:T(8,128)(2,1)}), bf16[128,1,48,384]{3,2,1,0:T(8,128)(2,1)}, u32[]{:S(2)}, u32[]{:S(2)}) %all-to-all-start.1) | async-done | bytes 4718624 | tf_op jit(solution)/shard_map/all_to_all | solution.py:25
  103.6 5.9 %all-to-all-start = ((bf16[128,1,48,384]{3,2,1,0:T(8,128)(2,1)}), bf16[128,1,48,384]{3,2,1,0:T(8,128)(2,1)}, u32[]{:S(2)}, u32[]{:S(2)}) async-start(bf16[128,1,48,384]{3,2,1,0:T(8,128)(2,1)} %copy.23), calls=%async_computation | async-start | bytes 9437184 | tf_op jit(solution)/shard_map/all_to_all | solution.py:25
  109.5 5.0 %copy.27 = bf16[4,1,32,48,384]{4,3,2,0,1:T(8,128)(2,1)} copy(bf16[4,1,32,48,384]{4,3,0,2,1:T(8,128)(2,1)} %bitcast.15) | data formatting | bytes 9437184 | tf_op jit(solution)/shard_map/transpose | solution.py:14
  114.5 6.6 %copy.28 = bf16[1,1536,4,384]{1,3,2,0:T(8,128)(2,1)} copy(bf16[1,1536,4,384]{3,1,2,0:T(8,128)(2,1)} %bitcast.89) | data formatting | bytes 9437184 | tf_op jit(solution)/shard_map/transpose | solution.py:14
  121.1 47.6 %all-to-all-done = bf16[128,1,48,384]{3,2,1,0:T(8,128)(2,1)} async-done(((bf16[128,1,48,384]{3,2,1,0:T(8,128)(2,1)}), bf16[128,1,48,384]{3,2,1,0:T(8,128)(2,1)}, u32[]{:S(2)}, u32[]{:S(2)}) %all-to-all-start) | async-done | bytes 4718624 | tf_op jit(solution)/shard_map/all_to_all | solution.py:25
  168.7 5.0 %copy.24 = bf16[4,1,32,48,384]{4,3,2,0,1:T(8,128)(2,1)} copy(bf16[4,1,32,48,384]{4,3,0,2,1:T(8,128)(2,1)} %bitcast.6) | data formatting | bytes 9437184 | tf_op jit(solution)/shard_map/transpose | solution.py:14
  173.7 6.7 %copy.25 = bf16[1,1536,4,384]{1,3,2,0:T(8,128)(2,1)} copy(bf16[1,1536,4,384]{3,1,2,0:T(8,128)(2,1)} %bitcast.90) | data formatting | bytes 9437184 | tf_op jit(solution)/shard_map/transpose | solution.py:14
  180.4 12.2 %convolution_convert_fusion = bf16[1536,1536]{1,0:T(8,128)(2,1)} fusion(bf16[1536,1536]{0,1:T(8,128)(2,1)} %bitcast.92, bf16[1536,1536]{0,1:T(8,128)(2,1)} %bitcast.91), kind=kOutput, calls=%fused_computation.19 | convolution fusion | flops 7250116608 | bytes 14155776 | tf_op jit(solution)/shard_map/cki,ckj->cij/dot_general | solution.py:56
  192.6 9.0 %reshape_transpose_reshape.3 = bf16[32,1,48,4,384]{4,3,2,0,1:T(4,128)(2,1)} reshape(bf16[1536,1536]{1,0:T(8,128)(2,1)} %convolution_convert_fusion) | data formatting | bytes 9437184 | tf_op jit(solution)/shard_map/reshape;transpose;reshape | solution.py:9
  201.6 0.0 copy-start.6
  201.6 5.4 %copy.29 = bf16[32,1,48,4,384]{4,2,3,0,1:T(8,128)(2,1)} copy(bf16[32,1,48,4,384]{4,3,2,0,1:T(4,128)(2,1)} %reshape_transpose_reshape.3) | data formatting | bytes 9437184 | tf_op jit(solution)/shard_map/reshape;transpose;reshape | solution.py:9
  207.1 5.9 %all-to-all-start.2 = ((bf16[128,1,48,384]{3,2,1,0:T(8,128)(2,1)}), bf16[128,1,48,384]{3,2,1,0:T(8,128)(2,1)}, u32[]{:S(2)}, u32[]{:S(2)}) async-start(bf16[128,1,48,384]{3,2,1,0:T(8,128)(2,1)} %bitcast.88), calls=%async_computation.2 | async-start | bytes 9437184 | tf_op jit(solution)/shard_map/all_to_all | solution.py:25
  212.9 0.0 copy-done.6
  213.0 0.1 reshape.80
  213.1 59.1 %all-to-all-done.2 = bf16[128,1,48,384]{3,2,1,0:T(8,128)(2,1)} async-done(((bf16[128,1,48,384]{3,2,1,0:T(8,128)(2,1)}), bf16[128,1,48,384]{3,2,1,0:T(8,128)(2,1)}, u32[]{:S(2)}, u32[]{:S(2)}) %all-to-all-start.2) | async-done | bytes 4718624 | tf_op jit(solution)/shard_map/all_to_all | solution.py:25
  272.2 0.0 copy-start.4
  272.2 3.1 %fusion.7 = f32[48,384]{1,0:T(8,128)S(1)} fusion(bf16[32,4,1,48,384]{4,3,1,0,2:T(8,128)(2,1)} %bitcast.25), kind=kLoop, calls=%fused_computation.11 | loop fusion | flops 4700160 | bytes 4792320 | tf_op jit(solution)/shard_map/reduce_sum | solution.py:72
  275.3 3.6 %fusion.10 = f32[48,384]{1,0:T(8,128)S(1)} fusion(bf16[32,4,1,48,384]{4,3,1,0,2:T(8,128)(2,1)} %bitcast.25, f32[48,384]{1,0:T(8,128)S(1)} %broadcast_multiply_fusion), kind=kLoop, calls=%fused_computation.14 | loop fusion | flops 9418752 | bytes 4866048 | tf_op jit(solution)/shard_map/reduce_sum | solution.py:73
  278.9 0.0 slice-start.2
  278.9 3.9 %fusion.13 = bf16[4,32,48,384]{3,2,0,1:T(8,128)(2,1)S(1)} fusion(bf16[32,4,1,48,384]{4,3,1,0,2:T(8,128)(2,1)} %bitcast.25, f32[4,32]{0,1:T(8,128)S(1)} %bitcast.93, f32[48,384]{1,0:T(8,128)S(1)} %add_rsqrt_fusion, f32[48,384]{1,0:T(8,128)S(1)} %broadcast_multiply_fusion), kind=kLoop, calls=%fused_computation.20 | loop fusion | flops 11796480 | bytes 9585152 | tf_op jit(solution)/shard_map/reshape.35
  282.8 0.0 copy-done.4
  282.8 0.0 slice-start.3
  282.9 0.0 copy-start.9
  282.9 5.4 %fusion.14 = f32[48,384,128,1]{2,1,3,0:T(8,128)S(1)} fusion(bf16[4,32,48,384]{3,2,0,1:T(8,128)(2,1)S(1)} %fusion.13, bf16[32,4,1,128]{3,1,0,2:T(4,128)(2,1)S(1)} %bitcast.94), kind=kOutput, calls=%fused_computation.21 | convolution fusion | flops 603979776 | bytes 14188544 | tf_op jit(solution)/shard_map/cij,cd->ijd/dot_general | solution.py:75
  288.3 0.0 slice-done.2
  288.3 0.0 slice-done.3
  288.3 0.0 copy-done.9
  288.3 0.0 copy-start.1
  288.3 9.6 %fusion.5 = bf16[48,384,128]{2,1,0:T(8,128)(2,1)} fusion(f32[48,384,128,1]{2,1,3,0:T(8,128)S(1)} %fusion.14, bf16[128,128]{1,0:T(8,128)(2,1)S(1)} %copy-done.9, bf16[48,384,128]{2,1,0:T(8,128)(2,1)S(1)} %bitcast.87, f32[128]{0:T(128)S(1)} %copy-done.5, f32[48,384]{1,0:T(8,128)S(1)} %add_rsqrt_fusion.1, f32[48,384]{1,0:T(8,128)S(1)} %broadcast_multiply_fusion.1), kind=kOutput, calls=%fused_computation.8 | convolution fusion | flops 627572736 | bytes 19055104 | tf_op jit(solution)/shard_map/ijd,de->ije/dot_general | solution.py:50
  297.9 0.0 copy-done.1
  (6 shorter events, 0.1 us)
Async XLA Ops:
  0.0 11.0 %copy-start = (bf16[128,128]{1,0:T(8,128)(2,1)S(1)}, bf16[128,128]{1,0:T(8,128)(2,1)}, u32[]{:S(2)}) copy-start(bf16[128,128]{1,0:T(8,128)(2,1)} %param.13) | copy-start | bytes 98308
  0.0 11.0 %copy-start.2 = (bf16[48,384,128]{2,1,0:T(8,128)(2,1)S(1)}, bf16[48,384,128]{2,1,0:T(8,128)(2,1)}, u32[]{:S(2)}) copy-start(bf16[48,384,128]{2,1,0:T(8,128)(2,1)} %param.9) | copy-start | bytes 14155780
  0.0 11.0 %copy-start.5 = (f32[128]{0:T(128)S(1)}, f32[128]{0:T(128)}, u32[]{:S(2)}) copy-start(f32[128]{0:T(128)} %param.10) | copy-start | bytes 1540
  11.0 5.1 %copy-start.7 = (bf16[128,128]{1,0:T(8,128)(2,1)S(1)}, bf16[128,128]{1,0:T(8,128)(2,1)}, u32[]{:S(2)}) copy-start(bf16[128,128]{1,0:T(8,128)(2,1)} %param.14) | copy-start | bytes 98308
  25.3 19.1 %copy-start.3 = (bf16[128,128]{1,0:T(8,128)(2,1)S(1)}, bf16[128,128]{1,0:T(8,128)(2,1)}, u32[]{:S(2)}) copy-start(bf16[128,128]{1,0:T(8,128)(2,1)} %param.11) | copy-start | bytes 98308
  32.5 21.4 %slice-start = ((s8[4718592]{0:T(1024)(128)(4,1)}), s8[524288]{0:T(1024)(128)(4,1)S(1)}, s32[]{:S(2)}) async-start(s8[4718592]{0:T(1024)(128)(4,1)} %bitcast.84), calls=%async_computation.3 | async-start | bytes 1048576
  32.5 71.1 %all-to-all-start.1 = ((bf16[128,1,48,384]{3,2,1,0:T(8,128)(2,1)}), bf16[128,1,48,384]{3,2,1,0:T(8,128)(2,1)}, u32[]{:S(2)}, u32[]{:S(2)}) async-start(bf16[128,1,48,384]{3,2,1,0:T(8,128)(2,1)} %copy.26), calls=%async_computation.1 | async-start | bytes 9437184 | tf_op jit(solution)/shard_map/all_to_all | solution.py:25
  44.4 9.5 %slice-start.1 = ((s8[4718592]{0:T(1024)(128)(4,1)}), s8[4194304]{0:T(1024)(128)(4,1)S(1)}, s32[]{:S(2)}) async-start(s8[4718592]{0:T(1024)(128)(4,1)} %bitcast.84), calls=%async_computation.4 | async-start | bytes 8388608
  44.4 9.5 %copy-start.8 = (bf16[128,128]{1,0:T(8,128)(2,1)S(1)}, bf16[128,128]{1,0:T(8,128)(2,1)}, u32[]{:S(2)}) copy-start(bf16[128,128]{1,0:T(8,128)(2,1)} %param.12) | copy-start | bytes 98308
  103.6 65.1 %all-to-all-start = ((bf16[128,1,48,384]{3,2,1,0:T(8,128)(2,1)}), bf16[128,1,48,384]{3,2,1,0:T(8,128)(2,1)}, u32[]{:S(2)}, u32[]{:S(2)}) async-start(bf16[128,1,48,384]{3,2,1,0:T(8,128)(2,1)} %copy.23), calls=%async_computation | async-start | bytes 9437184 | tf_op jit(solution)/shard_map/all_to_all | solution.py:25
  201.6 11.3 %copy-start.6 = (f32[128]{0:T(128)S(1)}, f32[128]{0:T(128)}, u32[]{:S(2)}) copy-start(f32[128]{0:T(128)} %param.17) | copy-start | bytes 1540
  207.1 65.1 %all-to-all-start.2 = ((bf16[128,1,48,384]{3,2,1,0:T(8,128)(2,1)}), bf16[128,1,48,384]{3,2,1,0:T(8,128)(2,1)}, u32[]{:S(2)}, u32[]{:S(2)}) async-start(bf16[128,1,48,384]{3,2,1,0:T(8,128)(2,1)} %bitcast.88), calls=%async_computation.2 | async-start | bytes 9437184 | tf_op jit(solution)/shard_map/all_to_all | solution.py:25
  272.2 10.7 %copy-start.4 = (bf16[128,128]{1,0:T(8,128)(2,1)S(1)}, bf16[128,128]{1,0:T(8,128)(2,1)}, u32[]{:S(2)}) copy-start(bf16[128,128]{1,0:T(8,128)(2,1)} %param.16) | copy-start | bytes 98308
  278.9 9.4 %slice-start.2 = ((s8[4718592]{0:T(1024)(128)(4,1)}), s8[524288]{0:T(1024)(128)(4,1)S(1)}, s32[]{:S(2)}) async-start(s8[4718592]{0:T(1024)(128)(4,1)} %bitcast.86), calls=%async_computation.5 | async-start | bytes 1048576
  282.8 5.4 %slice-start.3 = ((s8[4718592]{0:T(1024)(128)(4,1)}), s8[4194304]{0:T(1024)(128)(4,1)S(1)}, s32[]{:S(2)}) async-start(s8[4718592]{0:T(1024)(128)(4,1)} %bitcast.86), calls=%async_computation.6 | async-start | bytes 8388608
  282.9 5.4 %copy-start.9 = (bf16[128,128]{1,0:T(8,128)(2,1)S(1)}, bf16[128,128]{1,0:T(8,128)(2,1)}, u32[]{:S(2)}) copy-start(bf16[128,128]{1,0:T(8,128)(2,1)} %param.15) | copy-start | bytes 98308
  288.3 9.6 %copy-start.1 = (bf16[128,128]{1,0:T(8,128)(2,1)S(1)}, bf16[128,128]{1,0:T(8,128)(2,1)}, u32[]{:S(2)}) copy-start(bf16[128,128]{1,0:T(8,128)(2,1)} %param.13) | copy-start | bytes 98308
where the time goes:
time: 299 us; the launch traced here: 298 us
  waiting for transfers between devices  140 us (47%)
  matrix products  60.1 us (20%)
  local copies, waits for them, and re-layouts  52.1 us (17%)
  starting transfers between devices  23.7 us (8%)
  other arithmetic  21.6 us (7%)
    all_to_all x3, waiting for transfers between devices, one_exchange(): parts = lax.all_to_all(parts, axis, split_axis=0, concat_axis=0, tiled=True)  140 us
    dot_general x4, matrix products, project_major(): jnp.einsum('ijd,de->eij', normed, weight, preferred_element_type=jnp.floa...  32.9 us
    all_to_all x3, starting transfers between devices, one_exchange(): parts = lax.all_to_all(parts, axis, split_axis=0, concat_axis=0, tiled=True)  23.7 us
    transpose x4, local copies, waits for them, and re-layouts, laid_out(): parts = jnp.moveaxis(parts, 0, dim)  23.3 us
    another operation x2, local copies, waits for them, and re-layouts, cut_along(): array.reshape(*shape[:dim], count, shape[dim] // count, *shape[dim + 1:])  14.5 us
    another operation x2, local copies, waits for them, and re-layouts, one_exchange(): parts = parts.reshape(-1, *inside)  14.2 us
    dot_general x1, matrix products, local(): jnp.einsum('cki,ckj->cij', left_owned, right_owned, preferred_element_typ...  12.2 us
    dot_general x1, matrix products, local(): jnp.einsum('ijd,de->ije', normed, w_out_gate, preferred_element_type=jnp....  9.56 us
  transfers between devices with their start and end apart: 3, of which 3 were waited for; matrix products, arithmetic and copies ran while one was open for 13% of the time, Pallas kernels for 0%

commit v1 on v0

v1 whole, which is shorter than its diff:
```python
import jax
import jax.numpy as jnp
from jax import lax
from jax.experimental import pallas as pl
from jax.experimental.pallas import tpu as pltpu
from jax.sharding import PartitionSpec as P

LANES = 128
ROWS = 16
PITCH = 20
EPS = 1e-05
AXES = ("row", "col")


def sigmoid(x):
    return 0.5 * jnp.tanh(0.5 * x) + 0.5


def normed_rows(values, gain):
    values = values.astype(jnp.float32)
    inv = 1.0 / values.shape[-1]
    centred = values - jnp.sum(values, axis=-1, keepdims=True) * inv
    variance = jnp.sum(centred * centred, axis=-1, keepdims=True) * inv
    return (centred * lax.rsqrt(variance + EPS) * gain).astype(jnp.bfloat16)


def front_kernel(pair_ref, gain_ref, weight_ref, out_ref, turn_ref):
    channels = out_ref.shape[0]
    tiles = pair_ref.shape[1] // LANES
    gain = gain_ref[...]
    for i in range(ROWS):
        normed = normed_rows(pair_ref[i], gain)
        for side in range(2):
            weight = weight_ref[pl.ds(2 * side * channels, 2 * channels), :]
            both = lax.dot_general(
                weight, normed, (((1,), (1,)), ((), ())), preferred_element_type=jnp.float32
            )
            value = sigmoid(both[:channels]) * both[channels:]
            for t in range(tiles):
                turn_ref[side * tiles + t, pl.ds(i, channels, stride=PITCH), :] = value[
                    :, t * LANES : (t + 1) * LANES
                ]
    for side in range(2):
        for t in range(tiles):
            for c in range(channels):
                out_ref[c, side, :, t * LANES : (t + 1) * LANES] = turn_ref[
                    side * tiles + t, pl.ds(c * PITCH, ROWS), :
                ].astype(jnp.bfloat16)


def front(pair, gain, weight):
    height, width, channels = pair.shape
    return pl.pallas_call(
        front_kernel,
        grid=(height // ROWS,),
        in_specs=[
            pl.BlockSpec((ROWS, width, channels), lambda g: (g, 0, 0)),
            pl.BlockSpec((1, channels), lambda g: (0, 0)),
            pl.BlockSpec((4 * channels, channels), lambda g: (0, 0)),
        ],
        out_specs=pl.BlockSpec((channels, 2, ROWS, width), lambda g: (0, 0, g, 0)),
        out_shape=jax.ShapeDtypeStruct((channels, 2, height, width), jnp.bfloat16),
        scratch_shapes=[
            pltpu.VMEM((2 * width // LANES, channels * PITCH, LANES), jnp.float32)
        ],
        compiler_params=pltpu.CompilerParams(vmem_limit_bytes=58 * 2**20),
        name="front",
    )(pair, gain, weight)


def gate_kernel(pair_ref, gain_ref, weight_ref, out_ref):
    gain = gain_ref[...]
    for i in range(ROWS):
        normed = normed_rows(pair_ref[i], gain)
        out_ref[i] = sigmoid(
            jnp.dot(normed, weight_ref[...], preferred_element_type=jnp.float32)
        ).astype(out_ref.dtype)


def gate(pair, gain, weight):
    height, width, channels = pair.shape
    return pl.pallas_call(
        gate_kernel,
        grid=(height // ROWS,),
        in_specs=[
            pl.BlockSpec((ROWS, width, channels), lambda g: (g, 0, 0)),
            pl.BlockSpec((1, channels), lambda g: (0, 0)),
            pl.BlockSpec((channels, channels), lambda g: (0, 0)),
        ],
        out_specs=pl.BlockSpec((ROWS, width, channels), lambda g: (g, 0, 0)),
        out_shape=jax.ShapeDtypeStruct(pair.shape, jnp.bfloat16),
        cost_estimate=pl.CostEstimate(
            flops=2 * height * width * channels * channels,
            bytes_accessed=4 * height * width * channels,
            transcendentals=height * width * channels,
        ),
        name="gate",
    )(pair, gain, weight)


def middle_kernel(left_ref, right_ref, out_ref, turned_ref):
    block = out_ref.shape[0] * out_ref.shape[2]
    width = left_ref.shape[-1]
    g, h = pl.program_id(0), pl.program_id(1)
    tokens = turned_ref.shape[1]

    @pl.when(g == 0)
    def _():
        turned_ref[pl.ds(h * width, width), :] = left_ref[:, 0, 0].reshape(tokens, width).T

    product = jnp.dot(
        turned_ref[pl.ds(h * width, width), :],
        right_ref[:, 0, 0].reshape(tokens, width),
        preferred_element_type=jnp.float32,
    )
    out_ref[...] = product.astype(jnp.bfloat16).reshape(out_ref.shape)


def middle(owned):
    rows, cols, _, height, width = owned.shape
    per_block = width // height
    return pl.pallas_call(
        middle_kernel,
        grid=(cols, cols),
        in_specs=[
            pl.BlockSpec(
                (rows, 1, 1, height, width),
                lambda g, h: (0, jnp.where(g == 0, h, cols - 1), 0, 0, 0),
            ),
            pl.BlockSpec((rows, 1, 1, height, width), lambda g, h: (0, g, 1, 0, 0)),
        ],
        out_specs=pl.BlockSpec((per_block, 1, height, width), lambda g, h: (h, g, 0, 0)),
        out_shape=jax.ShapeDtypeStruct((rows, cols, height, width), jnp.bfloat16),
        scratch_shapes=[pltpu.VMEM((cols * width, rows * height), jnp.bfloat16)],
        compiler_params=pltpu.CompilerParams(vmem_limit_bytes=58 * 2**20),
        name="middle",
    )(owned, owned)


def finish_kernel(summed_ref, gain_ref, weight_ref, gating_ref, out_ref, turn_ref):
    channels = summed_ref.shape[0]
    tiles = summed_ref.shape[2] // LANES
    inv = 1.0 / channels
    for t in range(tiles):
        lanes = slice(t * LANES, (t + 1) * LANES)
        total = jnp.zeros((ROWS, LANES), jnp.float32)
        for c in range(channels):
            total = total + summed_ref[c, :, lanes].astype(jnp.float32)
        mean = total * inv
        total = jnp.zeros((ROWS, LANES), jnp.float32)
        for c in range(channels):
            centred = summed_ref[c, :, lanes].astype(jnp.float32) - mean
            total = total + centred * centred
        scale = lax.rsqrt(total * inv + EPS)
        for c in range(channels):
            centred = summed_ref[c, :, lanes].astype(jnp.float32) - mean
            turn_ref[t, pl.ds(c * PITCH, ROWS), :] = centred * scale * gain_ref[c]
    for i in range(ROWS):
        for t in range(tiles):
            scaled = turn_ref[t, pl.ds(i, channels, stride=PITCH), :].astype(jnp.bfloat16)
            projected = lax.dot_general(
                scaled, weight_ref[...], (((0,), (0,)), ((), ())), preferred_element_type=jnp.float32
            )
            lanes = slice(t * LANES, (t + 1) * LANES)
            out_ref[i, lanes, :] = (gating_ref[i, lanes, :].astype(jnp.float32) * projected).astype(
                jnp.bfloat16
            )


def finish(summed, gain, weight, gating):
    channels, height, width = summed.shape
    return pl.pallas_call(
        finish_kernel,
        grid=(height // ROWS,),
        in_specs=[
            pl.BlockSpec((channels, ROWS, width), lambda g: (0, g, 0)),
            pl.BlockSpec(memory_space=pltpu.SMEM),
            pl.BlockSpec((channels, channels), lambda g: (0, 0)),
            pl.BlockSpec((ROWS, width, channels), lambda g: (g, 0, 0)),
        ],
        out_specs=pl.BlockSpec((ROWS, width, channels), lambda g: (g, 0, 0)),
        out_shape=jax.ShapeDtypeStruct((height, width, channels), jnp.bfloat16),
        scratch_shapes=[pltpu.VMEM((width // LANES, channels * PITCH, LANES), jnp.float32)],
        compiler_params=pltpu.CompilerParams(vmem_limit_bytes=58 * 2**20),
        name="finish",
    )(summed, gain, weight, gating)


def local(pair, gain_in, w_a_gate, w_a, w_b_gate, w_b, w_out_gate, w_out, gain_out):
    rows, cols = lax.axis_size("row"), lax.axis_size("col")
    height, width, channels = pair.shape
    gain = gain_in.reshape(1, channels)
    weight = jnp.concatenate([w_a_gate, w_a, w_b_gate, w_b], axis=1).T
    both = front(pair, gain, weight)
    owned = lax.all_to_all(both, AXES, split_axis=0, concat_axis=0, tiled=True)
    gating = gate(pair, gain, w_out_gate)
    summed = middle(owned.reshape(rows, cols, 2, height, width))
    summed = summed.reshape(rows * cols, height, width)
    returned = lax.all_to_all(summed, AXES, split_axis=0, concat_axis=0, tiled=True)
    return finish(returned, gain_out, w_out, gating)


def solution(mesh):
    in_specs = (P("row", "col", None), P(), P(), P(), P(), P(), P(), P(), P())
    out_specs = P("row", "col", None)
    return jax.shard_map(local, mesh=mesh, in_specs=in_specs, out_specs=out_specs, check_vma=False)
```

time: 299 us -> 236 us (0.79)
  blocking collectives: 0 us -> 121 us
  waiting for transfers between devices: 140 us -> 49.4 us
  matrix products: 60.1 us -> 0 us
  Pallas kernels: 0 us -> 51.7 us
  local copies, waits for them, and re-layouts: 52.1 us -> 3.47 us
  other arithmetic: 21.6 us -> 0.68 us
  starting transfers between devices: 23.7 us -> 8.96 us
    all_to_all x0 -> x1, blocking collectives: none -> 121 us  [local(): owned = lax.all_to_all(both, AXES, split_axis=0, concat_axis=0, tiled=True)]
    all_to_all x3 -> x1, waiting for transfers between devices: 140 us -> 49.4 us  [local(): lax.all_to_all(summed, AXES, split_axis=0, concat_axis=0, tiled=True)]
    dot_general x7 -> x0, matrix products: 60.1 us -> none  [the longest x4 32.9 us: project_major(): jnp.einsum('ijd,de->eij', normed, weight, preferred_element_type=jnp.floa...]
    pallas_call x0 -> x4, Pallas kernels: none -> 51.7 us  [the longest x1 18.3 us: middle(): pl.pallas_call(middle_kernel, grid=(cols, cols), in_specs=[pl.BlockSpec((...]
    another operation x4 -> x0, local copies, waits for them, and re-layouts: 28.7 us -> none  [the longest x2 14.5 us: cut_along(): array.reshape(*shape[:dim], count, shape[dim] // count, *shape[dim + 1:])]
    transpose x4 -> x0, local copies, waits for them, and re-layouts: 23.3 us -> none  [laid_out(): parts = jnp.moveaxis(parts, 0, dim)]
    reduce_sum x4 -> x0, other arithmetic: 17.6 us -> none  [the longest x1 7.13 us: layer_norm_last(): variance = jnp.mean(centred * centred, axis=-1, keepdims=True)]
    all_to_all x3 -> x1, starting transfers between devices: 23.7 us -> 8.96 us  [local(): lax.all_to_all(summed, AXES, split_axis=0, concat_axis=0, tiled=True)]
  transfers between devices with their start and end apart: 3 -> 1, of which waited for: 3 -> 1; matrix products, arithmetic and copies ran while one was open for 13% -> 0% of each run, Pallas kernels for 0% -> 4%
where the time goes in v1:
time: 236 us
  blocking collectives  121 us (51%)
  Pallas kernels  51.7 us (22%)
  waiting for transfers between devices  49.4 us (21%)
  starting transfers between devices  8.96 us (4%)
  local copies, waits for them, and re-layouts  3.47 us (1%)
    all_to_all x1, blocking collectives, local(): owned = lax.all_to_all(both, AXES, split_axis=0, concat_axis=0, tiled=True)  121 us
    all_to_all x1, waiting for transfers between devices, local(): lax.all_to_all(summed, AXES, split_axis=0, concat_axis=0, tiled=True)  49.4 us
    pallas_call x1, Pallas kernels, middle(): pl.pallas_call(middle_kernel, grid=(cols, cols), in_specs=[pl.BlockSpec((...  18.3 us
    pallas_call x1, Pallas kernels, front(): pl.pallas_call(front_kernel, grid=(height // ROWS,), in_specs=[pl.BlockSp...  14.2 us
    pallas_call x1, Pallas kernels, gate(): pl.pallas_call(gate_kernel, grid=(height // ROWS,), in_specs=[pl.BlockSpe...  9.81 us
    pallas_call x1, Pallas kernels, finish(): pl.pallas_call(finish_kernel, grid=(height // ROWS,), in_specs=[pl.BlockS...  9.41 us
    all_to_all x1, starting transfers between devices, local(): lax.all_to_all(summed, AXES, split_axis=0, concat_axis=0, tiled=True)  8.96 us
  transfers between devices with their start and end apart: 1, of which 1 were waited for; matrix products, arithmetic and copies ran while one was open for 0% of the time, Pallas kernels for 4%

profile of v1, /device:TPU:1, one launch (start us, length us, event | category | flops | bytes accessed | tf_op | source)
XLA Modules:
  0.0 235.6 jit_solution(3622079574858022326)
XLA Ops:
  0.0 0.9 copy.10
  0.9 0.9 copy.11
  1.7 0.9 copy.12
  2.6 0.9 copy.13
  3.5 0.7 maximum_bitcast_fusion.weight_ref
  4.2 14.2 %front.1 = bf16[128,2,48,384]{3,2,1,0:T(8,128)(2,1)} custom-call(bf16[48,384,128]{2,1,0:T(8,128)(2,1)} %pair_ref.3, f32[1,128]{1,0:T(1,128)} %bitcast.8, bf16[512,128]{1,0:T(8,128)(2,1)} %maximum_bitcast_fusion.weight_ref), custom_call_target="tpu_custom_call" | custom-call | tf_op jit(solution)/shard_map/front/pallas_call | solution.py:53
  18.4 121.4 %all_to_all.10 = bf16[128,2,48,384]{3,2,1,0:T(8,128)(2,1)} all-to-all(bf16[128,2,48,384]{3,2,1,0:T(8,128)(2,1)} %front.1), channel_id=1, replica_groups=mesh['row'=32,'col'=4] {'row','col'}, dimensions={0} | all-to-all | bytes 18874368 | tf_op jit(solution)/shard_map/all_to_all | solution.py:195
  139.7 18.3 %middle.1 = bf16[32,4,48,384]{3,2,1,0:T(8,128)(2,1)} custom-call(bf16[32,4,2,48,384]{4,3,2,1,0:T(8,128)(2,1)} %bitcast.5, bf16[32,4,2,48,384]{4,3,2,1,0:T(8,128)(2,1)} %bitcast.6), custom_call_target="tpu_custom_call" | custom-call | tf_op jit(solution)/shard_map/middle/pallas_call | solution.py:122
  158.1 9.0 %all-to-all-start.1 = ((bf16[128,48,384]{2,1,0:T(8,128)(2,1)}), bf16[128,48,384]{2,1,0:T(8,128)(2,1)}, u32[]{:S(2)}, u32[]{:S(2)}) async-start(bf16[128,48,384]{2,1,0:T(8,128)(2,1)} %bitcast.7), calls=%async_computation.1 | async-start | bytes 9437184 | tf_op jit(solution)/shard_map/all_to_all | solution.py:199
  167.0 9.8 %gate.1.gating_ref = bf16[48,384,128]{2,1,0:T(8,128)(2,1)} custom-call(bf16[48,384,128]{2,1,0:T(8,128)(2,1)} %pair_ref.3, f32[1,128]{1,0:T(1,128)} %bitcast.9, bf16[128,128]{1,0:T(8,128)(2,1)} %weight_ref.2), custom_call_target="tpu_custom_call" | custom-call | flops 603979776 | bytes 9437184 | tf_op jit(solution)/shard_map/gate/pallas_call | solution.py:82
  176.9 49.4 %all-to-all-done.1.summed_ref = bf16[128,48,384]{2,1,0:T(8,128)(2,1)} async-done(((bf16[128,48,384]{2,1,0:T(8,128)(2,1)}), bf16[128,48,384]{2,1,0:T(8,128)(2,1)}, u32[]{:S(2)}, u32[]{:S(2)}) %all-to-all-start.1) | async-done | bytes 4718624 | tf_op jit(solution)/shard_map/all_to_all | solution.py:199
  226.2 9.4 %finish.1 = bf16[48,384,128]{2,1,0:T(8,128)(2,1)} custom-call(bf16[128,48,384]{2,1,0:T(8,128)(2,1)} %all-to-all-done.1.summed_ref, f32[128]{0:T(128)} %gain_ref.1, bf16[128,128]{1,0:T(8,128)(2,1)} %weight_ref.3, bf16[48,384,128]{2,1,0:T(8,128)(2,1)} %gate.1.gating_ref), custom_call_target="tpu_custom_call" | custom-call | tf_op jit(solution)/shard_map/finish/pallas_call | solution.py:172
Async XLA Ops:
  158.1 68.2 %all-to-all-start.1 = ((bf16[128,48,384]{2,1,0:T(8,128)(2,1)}), bf16[128,48,384]{2,1,0:T(8,128)(2,1)}, u32[]{:S(2)}, u32[]{:S(2)}) async-start(bf16[128,48,384]{2,1,0:T(8,128)(2,1)} %bitcast.7), calls=%async_computation.1 | async-start | bytes 9437184 | tf_op jit(solution)/shard_map/all_to_all | solution.py:199

commit v2 on v1

v2 whole, which is shorter than its diff:
```python
import jax
import jax.numpy as jnp
from jax import lax
from jax.experimental import pallas as pl
from jax.experimental.pallas import tpu as pltpu
from jax.sharding import PartitionSpec as P

LANES = 128
ROWS = 16
PITCH = 20
EPS = 1e-05
FETCH = 8
PARTS = 2
GROUP = 2
AXES = ("row", "col")


def sigmoid(x):
    return 0.5 * jnp.tanh(0.5 * x) + 0.5


def normed_rows(values, gain):
    values = values.astype(jnp.float32)
    inv = 1.0 / values.shape[-1]
    centred = values - jnp.sum(values, axis=-1, keepdims=True) * inv
    variance = jnp.sum(centred * centred, axis=-1, keepdims=True) * inv
    return (centred * lax.rsqrt(variance + EPS) * gain).astype(jnp.bfloat16)


def front_kernel(
    pair_ref, gain_any, ag_any, a_any, bg_any, b_any, out_ref,
    rows_ref, gain_ref, raw_ref, weight_ref, normed_ref, turn_refs, block_ref,
    small_sems, in_sems, out_sems,
):
    height, width, channels = rows_ref.shape
    blocks = height // ROWS
    tiles = width // LANES
    part = channels // PARTS

    def fetch(k):
        here = pl.ds(k * ROWS, ROWS)
        return pltpu.make_async_copy(pair_ref.at[here], rows_ref.at[here], in_sems.at[k])

    def give(k, side):
        return pltpu.make_async_copy(
            block_ref.at[k, side],
            out_ref.at[:, side, pl.ds(k * ROWS, ROWS), :],
            out_sems.at[k, side],
        )

    def normalise(g):
        for i in range(GROUP):
            normed_ref[g % 2, pl.ds(i * width, width), :] = normed_rows(
                rows_ref[g * GROUP + i], gain
            )

    def project(g):
        k, i = divmod(g * GROUP, ROWS)
        for side in range(2):
            for p in range(PARTS):
                both = lax.dot_general(
                    weight_ref[pl.ds((side * PARTS + p) * 2 * part, 2 * part), :],
                    normed_ref[g % 2],
                    (((1,), (1,)), ((), ())),
                    preferred_element_type=jnp.float32,
                )
                value = (jnp.tanh(both[:part]) + 1.0) * both[part:]
                for u in range(GROUP * tiles):
                    row, t = divmod(u, tiles)
                    turn_refs[
                        k % 2, side, t, pl.ds(p * part * PITCH + i + row, part, stride=PITCH), :
                    ] = value[:, u * LANES : (u + 1) * LANES]

    def pack(k, pieces):
        for u in pieces:
            side, c = divmod(u, channels)
            for t in range(tiles):
                block_ref[k, side, c, :, t * LANES : (t + 1) * LANES] = turn_refs[
                    k % 2, side, t, pl.ds(c * PITCH, ROWS), :
                ].astype(jnp.bfloat16)
            if c == channels - 1:
                give(k, side).start()

    small = [
        pltpu.make_async_copy(ref, raw_ref.at[n], small_sems.at[n])
        for n, ref in enumerate((ag_any, a_any, bg_any, b_any))
    ]
    small.append(pltpu.make_async_copy(gain_any, gain_ref, small_sems.at[4]))
    fetch(0).start()
    for copy in small:
        copy.start()
    for k in range(1, blocks):
        fetch(k).start()
    for copy in small:
        copy.wait()
    for side in range(2):
        for offset, n in ((0, 2 * side), (part, 2 * side + 1)):
            turned = (0.5 * raw_ref[n].astype(jnp.float32)).T.astype(jnp.bfloat16)
            for p in range(PARTS):
                weight_ref[
                    pl.ds((side * PARTS + p) * 2 * part + offset, part), :
                ] = turned[p * part : (p + 1) * part]
    gain = gain_ref[...]
    fetch(0).wait()
    normalise(0)
    groups = height // GROUP
    per_block = ROWS // GROUP
    share = 2 * channels // per_block
    for g in range(groups):
        if g + 1 < groups:
            if (g + 1) % per_block == 0:
                fetch((g + 1) // per_block).wait()
            normalise(g + 1)
        project(g)
        k, i = divmod(g, per_block)
        if k > 0:
            pack(k - 1, range(i * share, (i + 1) * share))
    pack(blocks - 1, range(2 * channels))
    for k in range(blocks):
        for side in range(2):
            give(k, side).wait()


def front(pair, gain, *weights):
    height, width, channels = pair.shape
    blocks = height // ROWS
    anywhere = pl.BlockSpec(memory_space=pl.ANY)
    return pl.pallas_call(
        front_kernel,
        in_specs=[anywhere] * 6,
        out_specs=anywhere,
        out_shape=jax.ShapeDtypeStruct((channels, 2, height, width), jnp.bfloat16),
        scratch_shapes=[
            pltpu.VMEM(pair.shape, jnp.bfloat16),
            pltpu.VMEM(gain.shape, jnp.float32),
            pltpu.VMEM((4, channels, channels), jnp.bfloat16),
            pltpu.VMEM((4 * channels, channels), jnp.bfloat16),
            pltpu.VMEM((2, GROUP * width, channels), jnp.bfloat16),
            pltpu.VMEM((2, 2, width // LANES, channels * PITCH, LANES), jnp.float32),
            pltpu.VMEM((blocks, 2, channels, ROWS, width), jnp.bfloat16),
            pltpu.SemaphoreType.DMA((5,)),
            pltpu.SemaphoreType.DMA((blocks,)),
            pltpu.SemaphoreType.DMA((blocks, 2)),
        ],
        compiler_params=pltpu.CompilerParams(vmem_limit_bytes=58 * 2**20),
        name="front",
    )(pair, gain, *weights)


def gate_kernel(pair_ref, gain_ref, weight_ref, out_ref):
    gain = gain_ref[...]
    for i in range(ROWS):
        normed = normed_rows(pair_ref[i], gain)
        out_ref[i] = sigmoid(
            jnp.dot(normed, weight_ref[...], preferred_element_type=jnp.float32)
        ).astype(out_ref.dtype)


def gate(pair, gain, weight):
    height, width, channels = pair.shape
    return pl.pallas_call(
        gate_kernel,
        grid=(height // ROWS,),
        in_specs=[
            pl.BlockSpec((ROWS, width, channels), lambda g: (g, 0, 0)),
            pl.BlockSpec((1, channels), lambda g: (0, 0)),
            pl.BlockSpec((channels, channels), lambda g: (0, 0)),
        ],
        out_specs=pl.BlockSpec((ROWS, width, channels), lambda g: (g, 0, 0)),
        out_shape=jax.ShapeDtypeStruct(pair.shape, jnp.bfloat16),
        cost_estimate=pl.CostEstimate(
            flops=2 * height * width * channels * channels,
            bytes_accessed=4 * height * width * channels,
            transcendentals=height * width * channels,
        ),
        name="gate",
    )(pair, gain, weight)


def middle_kernel(owned_ref, out_ref, left_ref, right_ref, turned_ref, joined_ref, result_ref, in_sems, out_sems):
    cols, rows, height, width = left_ref.shape
    tokens = rows * height
    half = cols // 2
    span = half * width
    part = rows // 2

    def fetch(side, q):
        target = (left_ref, right_ref)[side]
        return pltpu.make_async_copy(
            owned_ref.at[:, q, side], target.at[q], in_sems.at[side, q]
        )

    def give(m, q):
        here = result_ref.at[q, pl.ds(m * part, part)]
        return pltpu.make_async_copy(
            here, out_ref.at[pl.ds(m * part, part), q], out_sems.at[m, q]
        )

    def turn(m):
        for q in range(m * half, (m + 1) * half):
            fetch(0, q).wait()
            turned_ref[pl.ds(q * width, width), :] = left_ref[q].reshape(tokens, width).T

    for n in range(2):
        for side in range(2):
            for q in range(n * half, (n + 1) * half):
                fetch(side, q).start()
    turn(0)
    for n in range(2):
        for q in range(n * half, (n + 1) * half):
            fetch(1, q).wait()
            joined_ref[n, :, pl.ds((q - n * half) * width, width)] = right_ref[q].reshape(
                tokens, width
            )
        if n == 0:
            turn(1)
        for m in range(2):
            product = jnp.dot(
                turned_ref[pl.ds(m * span, span), :],
                joined_ref[n],
                preferred_element_type=jnp.float32,
            ).astype(jnp.bfloat16)
            for q in range(half):
                result_ref[n * half + q, pl.ds(m * part, part)] = product[
                    :, q * width : (q + 1) * width
                ].reshape(part, height, width)
                give(m, n * half + q).start()
    for n in range(2):
        for m in range(2):
            for q in range(half):
                give(m, n * half + q).wait()


def middle(owned):
    rows, cols, _, height, width = owned.shape
    tokens = rows * height
    return pl.pallas_call(
        middle_kernel,
        in_specs=[pl.BlockSpec(memory_space=pl.ANY)],
        out_specs=pl.BlockSpec(memory_space=pl.ANY),
        out_shape=jax.ShapeDtypeStruct((rows, cols, height, width), jnp.bfloat16),
        scratch_shapes=[
            pltpu.VMEM((cols, rows, height, width), jnp.bfloat16),
            pltpu.VMEM((cols, rows, height, width), jnp.bfloat16),
            pltpu.VMEM((cols * width, tokens), jnp.bfloat16),
            pltpu.VMEM((2, tokens, cols * width // 2), jnp.bfloat16),
            pltpu.VMEM((cols, rows, height, width), jnp.bfloat16),
            pltpu.SemaphoreType.DMA((2, cols)),
            pltpu.SemaphoreType.DMA((2, cols)),
        ],
        compiler_params=pltpu.CompilerParams(vmem_limit_bytes=58 * 2**20),
        name="middle",
    )(owned)


def finish_kernel(
    summed_ref, gain_any, weight_any, gating_ref, out_ref,
    block_ref, gates_ref, gain_ref, weight_ref, scaled_ref, turn_ref, result_ref,
    small_sems, in_sems, gate_sems, out_sems,
):
    height, width, channels = result_ref.shape
    blocks = height // ROWS
    tiles = width // LANES
    inv = 1.0 / channels

    def fetch(k):
        return pltpu.make_async_copy(
            summed_ref.at[:, pl.ds(k * ROWS, ROWS), :], block_ref.at[k], in_sems.at[k]
        )

    def fetch_gates(k):
        here = pl.ds(k * ROWS, ROWS)
        return pltpu.make_async_copy(gating_ref.at[here], gates_ref.at[here], gate_sems.at[k])

    def give(k):
        here = pl.ds(k * FETCH, FETCH)
        return pltpu.make_async_copy(result_ref.at[here], out_ref.at[here], out_sems.at[k])

    small = [
        pltpu.make_async_copy(gain_any, gain_ref, small_sems.at[0]),
        pltpu.make_async_copy(weight_any, weight_ref, small_sems.at[1]),
    ]
    fetch(0).start()
    for copy in small:
        copy.start()
    fetch_gates(0).start()
    for k in range(1, blocks):
        fetch(k).start()
        fetch_gates(k).start()
    for copy in small:
        copy.wait()
    scaled_ref[...] = (weight_ref[...].astype(jnp.float32) * gain_ref[...]).astype(jnp.bfloat16)

    def body(k, carry):
        fetch(k).wait()
        for t in range(tiles):
            lanes = slice(t * LANES, (t + 1) * LANES)
            totals = [jnp.zeros((ROWS, LANES), jnp.float32) for _ in range(4)]
            for c in range(channels):
                totals[c % 4] = totals[c % 4] + block_ref[k, c, :, lanes].astype(jnp.float32)
            mean = ((totals[0] + totals[1]) + (totals[2] + totals[3])) * inv
            totals = [jnp.zeros((ROWS, LANES), jnp.float32) for _ in range(4)]
            for c in range(channels):
                centred = block_ref[k, c, :, lanes].astype(jnp.float32) - mean
                turn_ref[t, pl.ds(c * PITCH, ROWS), :] = centred
                totals[c % 4] = totals[c % 4] + centred * centred
            variance = ((totals[0] + totals[1]) + (totals[2] + totals[3])) * inv
            turn_ref[t, pl.ds(channels * PITCH, ROWS), :] = lax.rsqrt(variance + EPS)
        fetch_gates(k).wait()
        for i in range(ROWS):
            scaled = jnp.concatenate(
                [
                    (
                        turn_ref[t, pl.ds(i, channels, stride=PITCH), :]
                        * turn_ref[t, pl.ds(channels * PITCH + i, 1), :]
                    ).astype(jnp.bfloat16)
                    for t in range(tiles)
                ],
                axis=1,
            )
            projected = lax.dot_general(
                scaled, scaled_ref[...], (((0,), (0,)), ((), ())), preferred_element_type=jnp.float32
            )
            row = k * ROWS + i
            result_ref[row] = (gates_ref[row].astype(jnp.float32) * projected).astype(jnp.bfloat16)
            if i % FETCH == FETCH - 1:
                give(k * (ROWS // FETCH) + i // FETCH).start()
        return carry

    lax.fori_loop(0, blocks, body, 0)
    for k in range(height // FETCH):
        give(k).wait()


def finish(summed, gain, weight, gating):
    channels, height, width = summed.shape
    blocks = height // ROWS
    anywhere = pl.BlockSpec(memory_space=pl.ANY)
    return pl.pallas_call(
        finish_kernel,
        in_specs=[anywhere] * 4,
        out_specs=anywhere,
        out_shape=jax.ShapeDtypeStruct((height, width, channels), jnp.bfloat16),
        scratch_shapes=[
            pltpu.VMEM((blocks, channels, ROWS, width), jnp.bfloat16),
            pltpu.VMEM((height, width, channels), jnp.bfloat16),
            pltpu.VMEM((channels, 1), jnp.float32),
            pltpu.VMEM((channels, channels), jnp.bfloat16),
            pltpu.VMEM((channels, channels), jnp.bfloat16),
            pltpu.VMEM((width // LANES, (channels + 1) * PITCH, LANES), jnp.float32),
            pltpu.VMEM((height, width, channels), jnp.bfloat16),
            pltpu.SemaphoreType.DMA((2,)),
            pltpu.SemaphoreType.DMA((blocks,)),
            pltpu.SemaphoreType.DMA((blocks,)),
            pltpu.SemaphoreType.DMA((height // FETCH,)),
        ],
        compiler_params=pltpu.CompilerParams(vmem_limit_bytes=58 * 2**20),
        name="finish",
    )(summed, gain.reshape(channels, 1), weight, gating)


def local(pair, gain_in, w_a_gate, w_a, w_b_gate, w_b, w_out_gate, w_out, gain_out):
    rows, cols = lax.axis_size("row"), lax.axis_size("col")
    height, width, channels = pair.shape
    gain = gain_in.reshape(1, channels)
    both = front(pair, gain, w_a_gate, w_a, w_b_gate, w_b)
    owned = lax.all_to_all(both, AXES, split_axis=0, concat_axis=0, tiled=True)
    gating = gate(pair, gain, w_out_gate)
    summed = middle(owned.reshape(rows, cols, 2, height, width))
    summed = summed.reshape(rows * cols, height, width)
    returned = lax.all_to_all(summed, AXES, split_axis=0, concat_axis=0, tiled=True)
    return finish(returned, gain_out, w_out, gating)


def solution(mesh):
    in_specs = (P("row", "col", None), P(), P(), P(), P(), P(), P(), P(), P())
    out_specs = P("row", "col", None)
    return jax.shard_map(local, mesh=mesh, in_specs=in_specs, out_specs=out_specs, check_vma=False)
```

time: 236 us -> 223 us (0.945)
  Pallas kernels: 51.7 us -> 42.2 us
  local copies, waits for them, and re-layouts: 3.47 us -> 0.74 us
    pallas_call x3, Pallas kernels: 41.9 us -> 32.4 us  [the longest x1 12.7 us: front(): pl.pallas_call(front_kernel, in_specs=[anywhere] * 6, out_specs=anywhere,...]
    unnamed x4 -> x2, local copies, waits for them, and re-layouts: 3.47 us -> 0.01 us
where the time goes in v2:
time: 223 us
  blocking collectives  121 us (54%)
  waiting for transfers between devices  48.6 us (22%)
  Pallas kernels  42.2 us (19%)
  starting transfers between devices  9.32 us (4%)
    all_to_all x1, blocking collectives, local(): owned = lax.all_to_all(both, AXES, split_axis=0, concat_axis=0, tiled=True)  121 us
    all_to_all x1, waiting for transfers between devices, local(): lax.all_to_all(summed, AXES, split_axis=0, concat_axis=0, tiled=True)  48.6 us
    pallas_call x1, Pallas kernels, front(): pl.pallas_call(front_kernel, in_specs=[anywhere] * 6, out_specs=anywhere,...  12.7 us
    pallas_call x1, Pallas kernels, middle(): pl.pallas_call(middle_kernel, in_specs=[pl.BlockSpec(memory_space=pl.ANY)...  12.2 us
    pallas_call x1, Pallas kernels, gate(): pl.pallas_call(gate_kernel, grid=(height // ROWS,), in_specs=[pl.BlockSpe...  9.81 us
    all_to_all x1, starting transfers between devices, local(): lax.all_to_all(summed, AXES, split_axis=0, concat_axis=0, tiled=True)  9.32 us
    pallas_call x1, Pallas kernels, finish(): pl.pallas_call(finish_kernel, in_specs=[anywhere] * 4, out_specs=anywhere...  7.54 us
  transfers between devices with their start and end apart: 1, of which 1 were waited for; matrix products, arithmetic and copies ran while one was open for 0% of the time, Pallas kernels for 4%

profile of v2, /device:TPU:1, one launch (start us, length us, event | category | flops | bytes accessed | tf_op | source)
XLA Modules:
  0.0 222.6 jit_solution(15894733321437556790)
XLA Ops:
  0.0 12.7 %front.1 = bf16[128,2,48,384]{3,2,1,0:T(8,128)(2,1)} custom-call(bf16[48,384,128]{2,1,0:T(8,128)(2,1)} %pair_ref.3, f32[1,128]{1,0:T(1,128)} %bitcast.6, bf16[128,128]{1,0:T(8,128)(2,1)} %ag_any.1, bf16[128,128]{1,0:T(8,128)(2,1)} %a_any.1, bf16[128,128]{1,0:T(8,128)(2,1)} %bg_any.1, bf16[128,128]{1,0:T(8,128)(2,1)} %b_any.1), custom_call_target="tpu_custom_call" | custom-call | tf_op jit(solution)/shard_map/front/pallas_call | solution.py:128
  12.7 121.5 %all_to_all.10 = bf16[128,2,48,384]{3,2,1,0:T(8,128)(2,1)} all-to-all(bf16[128,2,48,384]{3,2,1,0:T(8,128)(2,1)} %front.1), channel_id=1, replica_groups=mesh['row'=32,'col'=4] {'row','col'}, dimensions={0} | all-to-all | bytes 18874368 | tf_op jit(solution)/shard_map/all_to_all | solution.py:367
  134.2 12.2 %middle.1 = bf16[32,4,48,384]{3,2,1,0:T(8,128)(2,1)} custom-call(bf16[32,4,2,48,384]{4,3,2,1,0:T(8,128)(2,1)} %bitcast.4), custom_call_target="tpu_custom_call" | custom-call | tf_op jit(solution)/shard_map/middle/pallas_call | solution.py:237
  146.4 0.0 copy-start
  146.4 9.3 %all-to-all-start.1 = ((bf16[128,48,384]{2,1,0:T(8,128)(2,1)}), bf16[128,48,384]{2,1,0:T(8,128)(2,1)}, u32[]{:S(2)}, u32[]{:S(2)}) async-start(bf16[128,48,384]{2,1,0:T(8,128)(2,1)} %bitcast.5), calls=%async_computation.1 | async-start | bytes 9437184 | tf_op jit(solution)/shard_map/all_to_all | solution.py:371
  155.7 0.0 copy-done
  155.7 0.7 copy.10.gain_any
  156.5 9.8 %gate.1.gating_ref = bf16[48,384,128]{2,1,0:T(8,128)(2,1)} custom-call(bf16[48,384,128]{2,1,0:T(8,128)(2,1)} %pair_ref.3, f32[1,128]{1,0:T(1,128)} %bitcast.7, bf16[128,128]{1,0:T(8,128)(2,1)} %weight_ref.1), custom_call_target="tpu_custom_call" | custom-call | flops 603979776 | bytes 9437184 | tf_op jit(solution)/shard_map/gate/pallas_call | solution.py:161
  166.3 48.6 %all-to-all-done.1.summed_ref = bf16[128,48,384]{2,1,0:T(8,128)(2,1)} async-done(((bf16[128,48,384]{2,1,0:T(8,128)(2,1)}), bf16[128,48,384]{2,1,0:T(8,128)(2,1)}, u32[]{:S(2)}, u32[]{:S(2)}) %all-to-all-start.1) | async-done | bytes 4718624 | tf_op jit(solution)/shard_map/all_to_all | solution.py:371
  214.9 7.5 %finish.1 = bf16[48,384,128]{2,1,0:T(8,128)(2,1)} custom-call(bf16[128,48,384]{2,1,0:T(8,128)(2,1)} %all-to-all-done.1.summed_ref, f32[128,1]{1,0:T(8,128)} %copy.10.gain_any, bf16[128,128]{1,0:T(8,128)(2,1)} %weight_any.1, bf16[48,384,128]{2,1,0:T(8,128)(2,1)} %gate.1.gating_ref), custom_call_target="tpu_custom_call" | custom-call | tf_op jit(solution)/shard_map/finish/pallas_call | solution.py:339
Async XLA Ops:
  146.4 9.3 %copy-start = (f32[128]{0:T(128)S(1)}, f32[128]{0:T(128)}, u32[]{:S(2)}) copy-start(f32[128]{0:T(128)} %param.17) | copy-start | bytes 1540
  146.4 68.5 %all-to-all-start.1 = ((bf16[128,48,384]{2,1,0:T(8,128)(2,1)}), bf16[128,48,384]{2,1,0:T(8,128)(2,1)}, u32[]{:S(2)}, u32[]{:S(2)}) async-start(bf16[128,48,384]{2,1,0:T(8,128)(2,1)} %bitcast.5), calls=%async_computation.1 | async-start | bytes 9437184 | tf_op jit(solution)/shard_map/all_to_all | solution.py:371

commit v3 on v2

--- a/solution.py
+++ b/solution.py
@@ -10,6 +10,8 @@
 PITCH = 20
 EPS = 1e-05
 FETCH = 8
+SPLIT = 8
+PIECES = 2
 PARTS = 2
 GROUP = 2
 AXES = ("row", "col")
@@ -37,15 +39,25 @@
     tiles = width // LANES
     part = channels // PARTS
 
-    def fetch(k):
-        here = pl.ds(k * ROWS, ROWS)
-        return pltpu.make_async_copy(pair_ref.at[here], rows_ref.at[here], in_sems.at[k])
-
-    def give(k, side):
+    def fetch(k, u):
+        size = ROWS // PIECES
+        here = pl.ds(k * ROWS + u * size, size)
+        return pltpu.make_async_copy(pair_ref.at[here], rows_ref.at[here], in_sems.at[k, u])
+
+    def begin(k):
+        for u in range(PIECES):
+            fetch(k, u).start()
+
+    def arrive(k):
+        for u in range(PIECES):
+            fetch(k, u).wait()
+
+    def give(k, side, u):
+        some = pl.ds(u * channels // PIECES, channels // PIECES)
         return pltpu.make_async_copy(
-            block_ref.at[k, side],
-            out_ref.at[:, side, pl.ds(k * ROWS, ROWS), :],
-            out_sems.at[k, side],
+            block_ref.at[k, side, some],
+            out_ref.at[some, side, pl.ds(k * ROWS, ROWS), :],
+            out_sems.at[k, side, u],
         )
 
     def normalise(g):
@@ -78,19 +90,17 @@
                 block_ref[k, side, c, :, t * LANES : (t + 1) * LANES] = turn_refs[
                     k % 2, side, t, pl.ds(c * PITCH, ROWS), :
                 ].astype(jnp.bfloat16)
-            if c == channels - 1:
-                give(k, side).start()
+            if (c + 1) % (channels // PIECES) == 0:
+                give(k, side, c * PIECES // channels).start()
 
     small = [
         pltpu.make_async_copy(ref, raw_ref.at[n], small_sems.at[n])
         for n, ref in enumerate((ag_any, a_any, bg_any, b_any))
     ]
     small.append(pltpu.make_async_copy(gain_any, gain_ref, small_sems.at[4]))
-    fetch(0).start()
+    begin(0)
     for copy in small:
         copy.start()
-    for k in range(1, blocks):
-        fetch(k).start()
     for copy in small:
         copy.wait()
     for side in range(2):
@@ -101,7 +111,9 @@
                     pl.ds((side * PARTS + p) * 2 * part + offset, part), :
                 ] = turned[p * part : (p + 1) * part]
     gain = gain_ref[...]
-    fetch(0).wait()
+    arrive(0)
+    for k in range(1, blocks):
+        begin(k)
     normalise(0)
     groups = height // GROUP
     per_block = ROWS // GROUP
@@ -109,7 +121,7 @@
     for g in range(groups):
         if g + 1 < groups:
             if (g + 1) % per_block == 0:
-                fetch((g + 1) // per_block).wait()
+                arrive((g + 1) // per_block)
             normalise(g + 1)
         project(g)
         k, i = divmod(g, per_block)
@@ -118,7 +130,8 @@
     pack(blocks - 1, range(2 * channels))
     for k in range(blocks):
         for side in range(2):
-            give(k, side).wait()
+            for u in range(PIECES):
+                give(k, side, u).wait()
 
 
 def front(pair, gain, *weights):
@@ -139,8 +152,8 @@
             pltpu.VMEM((2, 2, width // LANES, channels * PITCH, LANES), jnp.float32),
             pltpu.VMEM((blocks, 2, channels, ROWS, width), jnp.bfloat16),
             pltpu.SemaphoreType.DMA((5,)),
-            pltpu.SemaphoreType.DMA((blocks,)),
-            pltpu.SemaphoreType.DMA((blocks, 2)),
+            pltpu.SemaphoreType.DMA((blocks, PIECES)),
+            pltpu.SemaphoreType.DMA((blocks, 2, PIECES)),
         ],
         compiler_params=pltpu.CompilerParams(vmem_limit_bytes=58 * 2**20),
         name="front",
@@ -181,7 +194,6 @@
     cols, rows, height, width = left_ref.shape
     tokens = rows * height
     half = cols // 2
-    span = half * width
     part = rows // 2
 
     def fetch(side, q):
@@ -196,35 +208,59 @@
             here, out_ref.at[pl.ds(m * part, part), q], out_sems.at[m, q]
         )
 
-    def turn(m):
-        for q in range(m * half, (m + 1) * half):
-            fetch(0, q).wait()
-            turned_ref[pl.ds(q * width, width), :] = left_ref[q].reshape(tokens, width).T
-
-    for n in range(2):
-        for side in range(2):
-            for q in range(n * half, (n + 1) * half):
-                fetch(side, q).start()
-    turn(0)
-    for n in range(2):
+    def turn(q):
+        turned_ref[pl.ds(q * width, width), :] = left_ref[q].reshape(tokens, width).T
+
+    def join(n):
         for q in range(n * half, (n + 1) * half):
-            fetch(1, q).wait()
             joined_ref[n, :, pl.ds((q - n * half) * width, width)] = right_ref[q].reshape(
                 tokens, width
             )
-        if n == 0:
-            turn(1)
-        for m in range(2):
-            product = jnp.dot(
-                turned_ref[pl.ds(m * span, span), :],
-                joined_ref[n],
-                preferred_element_type=jnp.float32,
-            ).astype(jnp.bfloat16)
-            for q in range(half):
-                result_ref[n * half + q, pl.ds(m * part, part)] = product[
-                    :, q * width : (q + 1) * width
-                ].reshape(part, height, width)
-                give(m, n * half + q).start()
+
+    def multiply(n, start, size):
+        product = jnp.dot(
+            turned_ref[pl.ds(start * width, size * width), :],
+            joined_ref[n],
+            preferred_element_type=jnp.float32,
+        ).astype(jnp.bfloat16)
+        each = part // half
+        for q in range(half):
+            result_ref[n * half + q, pl.ds(start * each, size * each)] = product[
+                :, q * width : (q + 1) * width
+            ].reshape(size * each, height, width)
+
+    fetch(0, 0).start()
+    for q in range(half):
+        fetch(1, q).start()
+    for q in range(1, cols):
+        fetch(0, q).start()
+    for q in range(half, cols):
+        fetch(1, q).start()
+    fetch(0, 0).wait()
+    turn(0)
+    for q in range(half):
+        fetch(1, q).wait()
+    fetch(0, 1).wait()
+    join(0)
+    turn(1)
+    multiply(0, 0, 1)
+    for q in range(half, cols):
+        fetch(0, q).wait()
+        fetch(1, q).wait()
+    turn(2)
+    multiply(0, 1, 1)
+    for q in range(half):
+        give(0, q).start()
+    turn(3)
+    join(1)
+    multiply(0, half, 1)
+    multiply(0, half + 1, 1)
+    for q in range(half):
+        give(1, q).start()
+    for m in range(2):
+        multiply(1, m * half, half)
+        for q in range(half, cols):
+            give(m, q).start()
     for n in range(2):
         for m in range(2):
             for q in range(half):
@@ -263,9 +299,10 @@
     tiles = width // LANES
     inv = 1.0 / channels
 
-    def fetch(k):
+    def fetch(k, u):
+        some = pl.ds(u * channels // SPLIT, channels // SPLIT)
         return pltpu.make_async_copy(
-            summed_ref.at[:, pl.ds(k * ROWS, ROWS), :], block_ref.at[k], in_sems.at[k]
+            summed_ref.at[some, pl.ds(k * ROWS, ROWS), :], block_ref.at[k, some], in_sems.at[k, u]
         )
 
     def fetch_gates(k):
@@ -280,19 +317,25 @@
         pltpu.make_async_copy(gain_any, gain_ref, small_sems.at[0]),
         pltpu.make_async_copy(weight_any, weight_ref, small_sems.at[1]),
     ]
-    fetch(0).start()
+    for u in range(SPLIT):
+        fetch(0, u).start()
     for copy in small:
         copy.start()
     fetch_gates(0).start()
-    for k in range(1, blocks):
-        fetch(k).start()
-        fetch_gates(k).start()
     for copy in small:
         copy.wait()
     scaled_ref[...] = (weight_ref[...].astype(jnp.float32) * gain_ref[...]).astype(jnp.bfloat16)
 
     def body(k, carry):
-        fetch(k).wait()
+        for u in range(SPLIT):
+            fetch(k, u).wait()
+
+        @pl.when(k < blocks - 1)
+        def _():
+            for u in range(SPLIT):
+                fetch(k + 1, u).start()
+            fetch_gates(k + 1).start()
+
         for t in range(tiles):
             lanes = slice(t * LANES, (t + 1) * LANES)
             totals = [jnp.zeros((ROWS, LANES), jnp.float32) for _ in range(4)]
@@ -350,7 +393,7 @@
             pltpu.VMEM((width // LANES, (channels + 1) * PITCH, LANES), jnp.float32),
             pltpu.VMEM((height, width, channels), jnp.bfloat16),
             pltpu.SemaphoreType.DMA((2,)),
-            pltpu.SemaphoreType.DMA((blocks,)),
+            pltpu.SemaphoreType.DMA((blocks, SPLIT)),
             pltpu.SemaphoreType.DMA((blocks,)),
             pltpu.SemaphoreType.DMA((height // FETCH,)),
         ],

time: 223 us -> 222 us (level)
  no operation moved by 1% of the time
where the time goes in v3:
time: 222 us
  blocking collectives  121 us (55%)
  waiting for transfers between devices  48.6 us (22%)
  Pallas kernels  41.3 us (19%)
  starting transfers between devices  9.32 us (4%)
    all_to_all x1, blocking collectives, local(): owned = lax.all_to_all(both, AXES, split_axis=0, concat_axis=0, tiled=True)  121 us
    all_to_all x1, waiting for transfers between devices, local(): lax.all_to_all(summed, AXES, split_axis=0, concat_axis=0, tiled=True)  48.6 us
    pallas_call x1, Pallas kernels, front(): pl.pallas_call(front_kernel, in_specs=[anywhere] * 6, out_specs=anywhere,...  12.5 us
    pallas_call x1, Pallas kernels, middle(): pl.pallas_call(middle_kernel, in_specs=[pl.BlockSpec(memory_space=pl.ANY)...  11.9 us
    pallas_call x1, Pallas kernels, gate(): pl.pallas_call(gate_kernel, grid=(height // ROWS,), in_specs=[pl.BlockSpe...  9.81 us
    all_to_all x1, starting transfers between devices, local(): lax.all_to_all(summed, AXES, split_axis=0, concat_axis=0, tiled=True)  9.32 us
    pallas_call x1, Pallas kernels, finish(): pl.pallas_call(finish_kernel, in_specs=[anywhere] * 4, out_specs=anywhere...  7.02 us
  transfers between devices with their start and end apart: 1, of which 1 were waited for; matrix products, arithmetic and copies ran while one was open for 0% of the time, Pallas kernels for 4%

profile of v3, /device:TPU:1, one launch (start us, length us, event | category | flops | bytes accessed | tf_op | source)
XLA Modules:
  0.0 221.6 jit_solution(9722346999659663414)
XLA Ops:
  0.0 12.5 %front.1 = bf16[128,2,48,384]{3,2,1,0:T(8,128)(2,1)} custom-call(bf16[48,384,128]{2,1,0:T(8,128)(2,1)} %pair_ref.3, f32[1,128]{1,0:T(1,128)} %bitcast.6, bf16[128,128]{1,0:T(8,128)(2,1)} %ag_any.1, bf16[128,128]{1,0:T(8,128)(2,1)} %a_any.1, bf16[128,128]{1,0:T(8,128)(2,1)} %bg_any.1, bf16[128,128]{1,0:T(8,128)(2,1)} %b_any.1), custom_call_target="tpu_custom_call" | custom-call | tf_op jit(solution)/shard_map/front/pallas_call | solution.py:141
  12.5 121.5 %all_to_all.10 = bf16[128,2,48,384]{3,2,1,0:T(8,128)(2,1)} all-to-all(bf16[128,2,48,384]{3,2,1,0:T(8,128)(2,1)} %front.1), channel_id=1, replica_groups=mesh['row'=32,'col'=4] {'row','col'}, dimensions={0} | all-to-all | bytes 18874368 | tf_op jit(solution)/shard_map/all_to_all | solution.py:410
  134.0 11.9 %middle.1 = bf16[32,4,48,384]{3,2,1,0:T(8,128)(2,1)} custom-call(bf16[32,4,2,48,384]{4,3,2,1,0:T(8,128)(2,1)} %bitcast.4), custom_call_target="tpu_custom_call" | custom-call | tf_op jit(solution)/shard_map/middle/pallas_call | solution.py:273
  145.9 0.0 copy-start
  145.9 9.3 %all-to-all-start.1 = ((bf16[128,48,384]{2,1,0:T(8,128)(2,1)}), bf16[128,48,384]{2,1,0:T(8,128)(2,1)}, u32[]{:S(2)}, u32[]{:S(2)}) async-start(bf16[128,48,384]{2,1,0:T(8,128)(2,1)} %bitcast.5), calls=%async_computation.1 | async-start | bytes 9437184 | tf_op jit(solution)/shard_map/all_to_all | solution.py:414
  155.3 0.0 copy-done
  155.3 0.7 copy.10.gain_any
  156.0 9.8 %gate.1.gating_ref = bf16[48,384,128]{2,1,0:T(8,128)(2,1)} custom-call(bf16[48,384,128]{2,1,0:T(8,128)(2,1)} %pair_ref.3, f32[1,128]{1,0:T(1,128)} %bitcast.7, bf16[128,128]{1,0:T(8,128)(2,1)} %weight_ref.1), custom_call_target="tpu_custom_call" | custom-call | flops 603979776 | bytes 9437184 | tf_op jit(solution)/shard_map/gate/pallas_call | solution.py:174
  165.8 48.6 %all-to-all-done.1.summed_ref = bf16[128,48,384]{2,1,0:T(8,128)(2,1)} async-done(((bf16[128,48,384]{2,1,0:T(8,128)(2,1)}), bf16[128,48,384]{2,1,0:T(8,128)(2,1)}, u32[]{:S(2)}, u32[]{:S(2)}) %all-to-all-start.1) | async-done | bytes 4718624 | tf_op jit(solution)/shard_map/all_to_all | solution.py:414
  214.5 7.0 %finish.1 = bf16[48,384,128]{2,1,0:T(8,128)(2,1)} custom-call(bf16[128,48,384]{2,1,0:T(8,128)(2,1)} %all-to-all-done.1.summed_ref, f32[128,1]{1,0:T(8,128)} %copy.10.gain_any, bf16[128,128]{1,0:T(8,128)(2,1)} %weight_any.1, bf16[48,384,128]{2,1,0:T(8,128)(2,1)} %gate.1.gating_ref), custom_call_target="tpu_custom_call" | custom-call | tf_op jit(solution)/shard_map/finish/pallas_call | solution.py:382
Async XLA Ops:
  145.9 9.3 %copy-start = (f32[128]{0:T(128)S(1)}, f32[128]{0:T(128)}, u32[]{:S(2)}) copy-start(f32[128]{0:T(128)} %param.17) | copy-start | bytes 1540
  145.9 68.5 %all-to-all-start.1 = ((bf16[128,48,384]{2,1,0:T(8,128)(2,1)}), bf16[128,48,384]{2,1,0:T(8,128)(2,1)}, u32[]{:S(2)}, u32[]{:S(2)}) async-start(bf16[128,48,384]{2,1,0:T(8,128)(2,1)} %bitcast.5), calls=%async_computation.1 | async-start | bytes 9437184 | tf_op jit(solution)/shard_map/all_to_all | solution.py:414

commit v4 on v3

--- a/solution.py
+++ b/solution.py
@@ -149,7 +149,7 @@
             pltpu.VMEM((4, channels, channels), jnp.bfloat16),
             pltpu.VMEM((4 * channels, channels), jnp.bfloat16),
             pltpu.VMEM((2, GROUP * width, channels), jnp.bfloat16),
-            pltpu.VMEM((2, 2, width // LANES, channels * PITCH, LANES), jnp.float32),
+            pltpu.VMEM((2, 2, width // LANES, (channels + 2) * PITCH, LANES), jnp.float32),
             pltpu.VMEM((blocks, 2, channels, ROWS, width), jnp.bfloat16),
             pltpu.SemaphoreType.DMA((5,)),
             pltpu.SemaphoreType.DMA((blocks, PIECES)),
@@ -194,7 +194,7 @@
     cols, rows, height, width = left_ref.shape
     tokens = rows * height
     half = cols // 2
-    part = rows // 2
+    part = rows // cols
 
     def fetch(side, q):
         target = (left_ref, right_ref)[side]
@@ -223,11 +223,13 @@
             joined_ref[n],
             preferred_element_type=jnp.float32,
         ).astype(jnp.bfloat16)
-        each = part // half
         for q in range(half):
-            result_ref[n * half + q, pl.ds(start * each, size * each)] = product[
+            result_ref[n * half + q, pl.ds(start * part, size * part)] = product[
                 :, q * width : (q + 1) * width
-            ].reshape(size * each, height, width)
+            ].reshape(size * part, height, width)
+        for q in range(half):
+            for m in range(start, start + size):
+                give(m, n * half + q).start()
 
     fetch(0, 0).start()
     for q in range(half):
@@ -249,20 +251,15 @@
         fetch(1, q).wait()
     turn(2)
     multiply(0, 1, 1)
-    for q in range(half):
-        give(0, q).start()
     turn(3)
     join(1)
     multiply(0, half, 1)
     multiply(0, half + 1, 1)
-    for q in range(half):
-        give(1, q).start()
-    for m in range(2):
-        multiply(1, m * half, half)
-        for q in range(half, cols):
-            give(m, q).start()
+    multiply(1, 0, half)
+    multiply(1, half, 1)
+    multiply(1, half + 1, 1)
     for n in range(2):
-        for m in range(2):
+        for m in range(cols):
             for q in range(half):
                 give(m, n * half + q).wait()
 
@@ -282,7 +279,7 @@
             pltpu.VMEM((2, tokens, cols * width // 2), jnp.bfloat16),
             pltpu.VMEM((cols, rows, height, width), jnp.bfloat16),
             pltpu.SemaphoreType.DMA((2, cols)),
-            pltpu.SemaphoreType.DMA((2, cols)),
+            pltpu.SemaphoreType.DMA((cols, cols)),
         ],
         compiler_params=pltpu.CompilerParams(vmem_limit_bytes=58 * 2**20),
         name="middle",
@@ -390,7 +387,7 @@
             pltpu.VMEM((channels, 1), jnp.float32),
             pltpu.VMEM((channels, channels), jnp.bfloat16),
             pltpu.VMEM((channels, channels), jnp.bfloat16),
-            pltpu.VMEM((width // LANES, (channels + 1) * PITCH, LANES), jnp.float32),
+            pltpu.VMEM((width // LANES, (channels + 2) * PITCH, LANES), jnp.float32),
             pltpu.VMEM((height, width, channels), jnp.bfloat16),
             pltpu.SemaphoreType.DMA((2,)),
             pltpu.SemaphoreType.DMA((blocks, SPLIT)),

time: 222 us -> 222 us (level)
  no operation moved by 1% of the time
where the time goes in v4:
time: 222 us
  blocking collectives  121 us (55%)
  waiting for transfers between devices  48.6 us (22%)
  Pallas kernels  41.2 us (19%)
  starting transfers between devices  9.32 us (4%)
    all_to_all x1, blocking collectives, local(): owned = lax.all_to_all(both, AXES, split_axis=0, concat_axis=0, tiled=True)  121 us
    all_to_all x1, waiting for transfers between devices, local(): lax.all_to_all(summed, AXES, split_axis=0, concat_axis=0, tiled=True)  48.6 us
    pallas_call x1, Pallas kernels, front(): pl.pallas_call(front_kernel, in_specs=[anywhere] * 6, out_specs=anywhere,...  12.5 us
    pallas_call x1, Pallas kernels, middle(): pl.pallas_call(middle_kernel, in_specs=[pl.BlockSpec(memory_space=pl.ANY)...  11.8 us
    pallas_call x1, Pallas kernels, gate(): pl.pallas_call(gate_kernel, grid=(height // ROWS,), in_specs=[pl.BlockSpe...  9.81 us
    all_to_all x1, starting transfers between devices, local(): lax.all_to_all(summed, AXES, split_axis=0, concat_axis=0, tiled=True)  9.32 us
    pallas_call x1, Pallas kernels, finish(): pl.pallas_call(finish_kernel, in_specs=[anywhere] * 4, out_specs=anywhere...  7.02 us
  transfers between devices with their start and end apart: 1, of which 1 were waited for; matrix products, arithmetic and copies ran while one was open for 0% of the time, Pallas kernels for 4%

profile of v4, /device:TPU:1, one launch (start us, length us, event | category | flops | bytes accessed | tf_op | source)
XLA Modules:
  0.0 221.5 jit_solution(11611953138607127360)
XLA Ops:
  0.0 12.5 %front.1 = bf16[128,2,48,384]{3,2,1,0:T(8,128)(2,1)} custom-call(bf16[48,384,128]{2,1,0:T(8,128)(2,1)} %pair_ref.3, f32[1,128]{1,0:T(1,128)} %bitcast.6, bf16[128,128]{1,0:T(8,128)(2,1)} %ag_any.1, bf16[128,128]{1,0:T(8,128)(2,1)} %a_any.1, bf16[128,128]{1,0:T(8,128)(2,1)} %bg_any.1, bf16[128,128]{1,0:T(8,128)(2,1)} %b_any.1), custom_call_target="tpu_custom_call" | custom-call | tf_op jit(solution)/shard_map/front/pallas_call | solution.py:141
  12.5 121.5 %all_to_all.10 = bf16[128,2,48,384]{3,2,1,0:T(8,128)(2,1)} all-to-all(bf16[128,2,48,384]{3,2,1,0:T(8,128)(2,1)} %front.1), channel_id=1, replica_groups=mesh['row'=32,'col'=4] {'row','col'}, dimensions={0} | all-to-all | bytes 18874368 | tf_op jit(solution)/shard_map/all_to_all | solution.py:407
  134.0 11.8 %middle.1 = bf16[32,4,48,384]{3,2,1,0:T(8,128)(2,1)} custom-call(bf16[32,4,2,48,384]{4,3,2,1,0:T(8,128)(2,1)} %bitcast.4), custom_call_target="tpu_custom_call" | custom-call | tf_op jit(solution)/shard_map/middle/pallas_call | solution.py:270
  145.8 0.0 copy-start
  145.8 9.3 %all-to-all-start.1 = ((bf16[128,48,384]{2,1,0:T(8,128)(2,1)}), bf16[128,48,384]{2,1,0:T(8,128)(2,1)}, u32[]{:S(2)}, u32[]{:S(2)}) async-start(bf16[128,48,384]{2,1,0:T(8,128)(2,1)} %bitcast.5), calls=%async_computation.1 | async-start | bytes 9437184 | tf_op jit(solution)/shard_map/all_to_all | solution.py:411
  155.2 0.0 copy-done
  155.2 0.7 copy.10.gain_any
  155.9 9.8 %gate.1.gating_ref = bf16[48,384,128]{2,1,0:T(8,128)(2,1)} custom-call(bf16[48,384,128]{2,1,0:T(8,128)(2,1)} %pair_ref.3, f32[1,128]{1,0:T(1,128)} %bitcast.7, bf16[128,128]{1,0:T(8,128)(2,1)} %weight_ref.1), custom_call_target="tpu_custom_call" | custom-call | flops 603979776 | bytes 9437184 | tf_op jit(solution)/shard_map/gate/pallas_call | solution.py:174
  165.7 48.6 %all-to-all-done.1.summed_ref = bf16[128,48,384]{2,1,0:T(8,128)(2,1)} async-done(((bf16[128,48,384]{2,1,0:T(8,128)(2,1)}), bf16[128,48,384]{2,1,0:T(8,128)(2,1)}, u32[]{:S(2)}, u32[]{:S(2)}) %all-to-all-start.1) | async-done | bytes 4718624 | tf_op jit(solution)/shard_map/all_to_all | solution.py:411
  214.4 7.0 %finish.1 = bf16[48,384,128]{2,1,0:T(8,128)(2,1)} custom-call(bf16[128,48,384]{2,1,0:T(8,128)(2,1)} %all-to-all-done.1.summed_ref, f32[128,1]{1,0:T(8,128)} %copy.10.gain_any, bf16[128,128]{1,0:T(8,128)(2,1)} %weight_any.1, bf16[48,384,128]{2,1,0:T(8,128)(2,1)} %gate.1.gating_ref), custom_call_target="tpu_custom_call" | custom-call | tf_op jit(solution)/shard_map/finish/pallas_call | solution.py:379
Async XLA Ops:
  145.8 9.3 %copy-start = (f32[128]{0:T(128)S(1)}, f32[128]{0:T(128)}, u32[]{:S(2)}) copy-start(f32[128]{0:T(128)} %param.17) | copy-start | bytes 1540
  145.8 68.5 %all-to-all-start.1 = ((bf16[128,48,384]{2,1,0:T(8,128)(2,1)}), bf16[128,48,384]{2,1,0:T(8,128)(2,1)}, u32[]{:S(2)}, u32[]{:S(2)}) async-start(bf16[128,48,384]{2,1,0:T(8,128)(2,1)} %bitcast.5), calls=%async_computation.1 | async-start | bytes 9437184 | tf_op jit(solution)/shard_map/all_to_all | solution.py:411

commit v5 on v4

--- a/solution.py
+++ b/solution.py
@@ -406,6 +406,7 @@
     both = front(pair, gain, w_a_gate, w_a, w_b_gate, w_b)
     owned = lax.all_to_all(both, AXES, split_axis=0, concat_axis=0, tiled=True)
     gating = gate(pair, gain, w_out_gate)
+    owned, gating = lax.optimization_barrier((owned, gating))
     summed = middle(owned.reshape(rows, cols, 2, height, width))
     summed = summed.reshape(rows * cols, height, width)
     returned = lax.all_to_all(summed, AXES, split_axis=0, concat_axis=0, tiled=True)

time: 222 us -> 230 us (1.036)
  waiting for transfers between devices: 48.6 us -> 170 us
  blocking collectives: 121 us -> 0 us
  starting transfers between devices: 9.32 us -> 17.4 us
    all_to_all x1 -> x0, blocking collectives: 121 us -> none  [local(): owned = lax.all_to_all(both, AXES, split_axis=0, concat_axis=0, tiled=True)]
    all_to_all x0 -> x1, waiting for transfers between devices: none -> 112 us  [local(): owned = lax.all_to_all(both, AXES, split_axis=0, concat_axis=0, tiled=True)]
    all_to_all x0 -> x1, starting transfers between devices: none -> 11.9 us  [local(): owned = lax.all_to_all(both, AXES, split_axis=0, concat_axis=0, tiled=True)]
    all_to_all x1, waiting for transfers between devices: 48.6 us -> 58.6 us  [local(): lax.all_to_all(summed, AXES, split_axis=0, concat_axis=0, tiled=True)]
    all_to_all x1, starting transfers between devices: 9.32 us -> 5.49 us  [local(): lax.all_to_all(summed, AXES, split_axis=0, concat_axis=0, tiled=True)]
  transfers between devices with their start and end apart: 1 -> 2, of which waited for: 1 -> 2; matrix products, arithmetic and copies ran while one was open for 0% -> 0% of each run, Pallas kernels for 4% -> 4%
where the time goes in v5:
time: 230 us
  waiting for transfers between devices  170 us (74%)
  Pallas kernels  41.1 us (18%)
  starting transfers between devices  17.4 us (8%)
    all_to_all x1, waiting for transfers between devices, local(): owned = lax.all_to_all(both, AXES, split_axis=0, concat_axis=0, tiled=True)  112 us
    all_to_all x1, waiting for transfers between devices, local(): lax.all_to_all(summed, AXES, split_axis=0, concat_axis=0, tiled=True)  58.6 us
    pallas_call x1, Pallas kernels, front(): pl.pallas_call(front_kernel, in_specs=[anywhere] * 6, out_specs=anywhere,...  12.4 us
    all_to_all x1, starting transfers between devices, local(): owned = lax.all_to_all(both, AXES, split_axis=0, concat_axis=0, tiled=True)  11.9 us
    pallas_call x1, Pallas kernels, middle(): pl.pallas_call(middle_kernel, in_specs=[pl.BlockSpec(memory_space=pl.ANY)...  11.8 us
    pallas_call x1, Pallas kernels, gate(): pl.pallas_call(gate_kernel, grid=(height // ROWS,), in_specs=[pl.BlockSpe...  9.8 us
    pallas_call x1, Pallas kernels, finish(): pl.pallas_call(finish_kernel, in_specs=[anywhere] * 4, out_specs=anywhere...  7.05 us
    all_to_all x1, starting transfers between devices, local(): lax.all_to_all(summed, AXES, split_axis=0, concat_axis=0, tiled=True)  5.49 us
  transfers between devices with their start and end apart: 2, of which 2 were waited for; matrix products, arithmetic and copies ran while one was open for 0% of the time, Pallas kernels for 4%

profile of v5, /device:TPU:1, one launch (start us, length us, event | category | flops | bytes accessed | tf_op | source)
XLA Modules:
  0.0 229.7 jit_solution(15856584924116561870)
XLA Ops:
  0.0 12.4 %front.1 = bf16[128,2,48,384]{3,2,1,0:T(8,128)(2,1)} custom-call(bf16[48,384,128]{2,1,0:T(8,128)(2,1)} %pair_ref.3, f32[1,128]{1,0:T(1,128)} %bitcast.5, bf16[128,128]{1,0:T(8,128)(2,1)} %ag_any.1, bf16[128,128]{1,0:T(8,128)(2,1)} %a_any.1, bf16[128,128]{1,0:T(8,128)(2,1)} %bg_any.1, bf16[128,128]{1,0:T(8,128)(2,1)} %b_any.1), custom_call_target="tpu_custom_call" | custom-call | tf_op jit(solution)/shard_map/front/pallas_call | solution.py:141
  12.4 11.9 %all-to-all-start = ((bf16[128,2,48,384]{3,2,1,0:T(8,128)(2,1)}), bf16[128,2,48,384]{3,2,1,0:T(8,128)(2,1)}, u32[]{:S(2)}, u32[]{:S(2)}) async-start(bf16[128,2,48,384]{3,2,1,0:T(8,128)(2,1)} %front.1), calls=%async_computation | async-start | bytes 18874368 | tf_op jit(solution)/shard_map/all_to_all | solution.py:407
  24.4 9.8 %gate.1.gating_ref = bf16[48,384,128]{2,1,0:T(8,128)(2,1)} custom-call(bf16[48,384,128]{2,1,0:T(8,128)(2,1)} %pair_ref.3, f32[1,128]{1,0:T(1,128)} %bitcast.6, bf16[128,128]{1,0:T(8,128)(2,1)} %weight_ref.1), custom_call_target="tpu_custom_call" | custom-call | flops 603979776 | bytes 9437184 | tf_op jit(solution)/shard_map/gate/pallas_call | solution.py:174
  34.2 111.7 %all-to-all-done = bf16[128,2,48,384]{3,2,1,0:T(8,128)(2,1)} async-done(((bf16[128,2,48,384]{3,2,1,0:T(8,128)(2,1)}), bf16[128,2,48,384]{3,2,1,0:T(8,128)(2,1)}, u32[]{:S(2)}, u32[]{:S(2)}) %all-to-all-start) | async-done | bytes 9437216 | tf_op jit(solution)/shard_map/all_to_all | solution.py:407
  145.8 11.8 %middle.1 = bf16[32,4,48,384]{3,2,1,0:T(8,128)(2,1)} custom-call(bf16[32,4,2,48,384]{4,3,2,1,0:T(8,128)(2,1)} %bitcast.1.owned_ref), custom_call_target="tpu_custom_call" | custom-call | tf_op jit(solution)/shard_map/middle/pallas_call | solution.py:270
  157.7 0.0 copy-start
  157.7 5.5 %all-to-all-start.1 = ((bf16[128,48,384]{2,1,0:T(8,128)(2,1)}), bf16[128,48,384]{2,1,0:T(8,128)(2,1)}, u32[]{:S(2)}, u32[]{:S(2)}) async-start(bf16[128,48,384]{2,1,0:T(8,128)(2,1)} %bitcast.4), calls=%async_computation.1 | async-start | bytes 9437184 | tf_op jit(solution)/shard_map/all_to_all | solution.py:412
  163.2 0.0 copy-done
  163.2 0.7 copy.10.gain_any
  163.9 58.6 %all-to-all-done.1.summed_ref = bf16[128,48,384]{2,1,0:T(8,128)(2,1)} async-done(((bf16[128,48,384]{2,1,0:T(8,128)(2,1)}), bf16[128,48,384]{2,1,0:T(8,128)(2,1)}, u32[]{:S(2)}, u32[]{:S(2)}) %all-to-all-start.1) | async-done | bytes 4718624 | tf_op jit(solution)/shard_map/all_to_all | solution.py:412
  222.5 7.0 %finish.1 = bf16[48,384,128]{2,1,0:T(8,128)(2,1)} custom-call(bf16[128,48,384]{2,1,0:T(8,128)(2,1)} %all-to-all-done.1.summed_ref, f32[128,1]{1,0:T(8,128)} %copy.10.gain_any, bf16[128,128]{1,0:T(8,128)(2,1)} %weight_any.1, bf16[48,384,128]{2,1,0:T(8,128)(2,1)} %gate.1.gating_ref), custom_call_target="tpu_custom_call" | custom-call | tf_op jit(solution)/shard_map/finish/pallas_call | solution.py:379
Async XLA Ops:
  12.4 133.4 %all-to-all-start = ((bf16[128,2,48,384]{3,2,1,0:T(8,128)(2,1)}), bf16[128,2,48,384]{3,2,1,0:T(8,128)(2,1)}, u32[]{:S(2)}, u32[]{:S(2)}) async-start(bf16[128,2,48,384]{3,2,1,0:T(8,128)(2,1)} %front.1), calls=%async_computation | async-start | bytes 18874368 | tf_op jit(solution)/shard_map/all_to_all | solution.py:407
  157.7 5.5 %copy-start = (f32[128]{0:T(128)S(1)}, f32[128]{0:T(128)}, u32[]{:S(2)}) copy-start(f32[128]{0:T(128)} %param.17) | copy-start | bytes 1540
  157.7 64.8 %all-to-all-start.1 = ((bf16[128,48,384]{2,1,0:T(8,128)(2,1)}), bf16[128,48,384]{2,1,0:T(8,128)(2,1)}, u32[]{:S(2)}, u32[]{:S(2)}) async-start(bf16[128,48,384]{2,1,0:T(8,128)(2,1)} %bitcast.4), calls=%async_computation.1 | async-start | bytes 9437184 | tf_op jit(solution)/shard_map/all_to_all | solution.py:412
